TPU v7x, 8 devices: a whole 2x2x1 slice. The times are simulated.
8 devices in a mesh: data: 1 (over z), dap: 8 (over y, x, core).
Axes of the slice: x: 2, y: 2, z: 1, core: 2. Of those that a mesh axis runs over, the one named last changes fastest.
Arguments:
- pair_act: float32 [512, 512, 128], P(('data', 'dap'))
- pair_mask: int32 [512, 512], P(('data', 'dap'))
- grad_out: float32 [512, 512, 128], P(('data', 'dap'))
- ln_pair: bfloat16 [2, 2, 128], replicated
- w_in: bfloat16 [2, 128, 640], replicated
- ln_tri: bfloat16 [2, 2, 128], replicated
- w_out: bfloat16 [2, 128, 128], replicated
Outputs:
- output 1: float32 [512, 512, 128], P(('data', 'dap'))
- output 2: float32 [2, 2, 128], P('data')
- output 3: float32 [2, 128, 640], P('data')
- output 4: float32 [2, 2, 128], P('data')
- output 5: float32 [2, 128, 128], P('data')
All inputs are finite; a program needn't handle non-finite values.
Results may differ from a plain program's by a relative error of at most 0.0135825.
Values are sent between devices in bfloat16 or wider.
A program may use at most 1 GiB of HBM per device.

v0:
```python
import jax
import jax.numpy as jnp
from jax import lax
from jax.sharding import PartitionSpec as P

LN_EPS = 1e-5


def layer_norm(values, gain_vec, bias_vec):
    mean_val = jnp.mean(values, axis=-1, keepdims=True)
    centred = values - mean_val
    variance = jnp.mean(centred * centred, axis=-1, keepdims=True)
    return centred * lax.rsqrt(variance + LN_EPS) * gain_vec + bias_vec


def project_rows(row_vals, mask_rows, ln_pair, w_in):
    hidden = (w_in.shape[1] - row_vals.shape[2]) // 4
    normed_f, ln_back = jax.vjp(layer_norm, row_vals, ln_pair[0].astype(jnp.float32), ln_pair[1].astype(jnp.float32))
    normed = normed_f.astype(jnp.bfloat16)
    proj_all = jnp.einsum('ijc,cd->ijd', normed, w_in, preferred_element_type=jnp.float32)
    mask_f = mask_rows.astype(jnp.float32)[:, :, None]
    a_lin = proj_all[:, :, :hidden]
    a_sig = jax.nn.sigmoid(proj_all[:, :, hidden:2 * hidden])
    b_lin = proj_all[:, :, 2 * hidden:3 * hidden]
    b_sig = jax.nn.sigmoid(proj_all[:, :, 3 * hidden:4 * hidden])
    gate_act = jax.nn.sigmoid(proj_all[:, :, 4 * hidden:])
    left_act = (mask_f * a_sig * a_lin).astype(jnp.bfloat16)
    right_act = (mask_f * b_sig * b_lin).astype(jnp.bfloat16)
    saved = (normed, ln_back, mask_f, a_lin, a_sig, b_lin, b_sig)
    return saved, left_act, right_act, gate_act


def project_back(saved, d_left, d_right, d_gate_pre, w_in):
    normed, ln_back, mask_f, a_lin, a_sig, b_lin, b_sig = saved
    grad_a = d_left.astype(jnp.float32) * mask_f
    grad_b = d_right.astype(jnp.float32) * mask_f
    d_cat = jnp.concatenate([grad_a * a_sig, grad_a * a_lin * a_sig * (1.0 - a_sig),
                             grad_b * b_sig, grad_b * b_lin * b_sig * (1.0 - b_sig),
                             d_gate_pre], axis=-1).astype(jnp.bfloat16)
    d_normed = jnp.einsum('ijd,cd->ijc', d_cat, w_in, preferred_element_type=jnp.float32)
    d_rows, d_gain, d_bias = ln_back(d_normed.astype(jnp.bfloat16).astype(jnp.float32))
    d_w_in = jnp.einsum('ijc,ijd->cd', normed, d_cat, preferred_element_type=jnp.float32)
    return d_rows, jnp.stack([d_gain, d_bias]), d_w_in


def finish_rows(tri_sum, ln_tri, w_out):
    norm_f, tri_back = jax.vjp(layer_norm, tri_sum, ln_tri[0].astype(jnp.float32), ln_tri[1].astype(jnp.float32))
    tri_norm = norm_f.astype(jnp.bfloat16)
    proj_out = jnp.einsum('ijc,cd->ijd', tri_norm, w_out, preferred_element_type=jnp.float32)
    return (tri_norm, tri_back, proj_out)


def finish_back(saved, gate_act, d_new, w_out):
    tri_norm, tri_back, proj_out = saved
    d_gate_pre = d_new * proj_out * gate_act * (1.0 - gate_act)
    d_proj = (d_new * gate_act).astype(jnp.bfloat16)
    d_w_out = jnp.einsum('ijc,ijd->cd', tri_norm, d_proj, preferred_element_type=jnp.float32)
    d_norm = jnp.einsum('ijd,cd->ijc', d_proj, w_out, preferred_element_type=jnp.float32)
    d_tri, d_gain, d_bias = tri_back(d_norm.astype(jnp.bfloat16).astype(jnp.float32))
    return d_tri.astype(jnp.bfloat16), d_gate_pre, d_w_out, jnp.stack([d_gain, d_bias])


def solution(mesh):
    row_spec = P(('data', 'dap'))
    grad_spec = P('data')

    def device_body(pair_act, pair_mask, grad_out, ln_pair, w_in, ln_tri, w_out):
        out_saved, out_left, out_right, out_gate = project_rows(pair_act, pair_mask, ln_pair[0], w_in[0])
        out_right_all = lax.all_gather(out_right, 'dap', axis=0, tiled=True)
        out_tri = jnp.einsum('ikc,jkc->ijc', out_left, out_right_all, preferred_element_type=jnp.float32)
        out_fin = finish_rows(out_tri, ln_tri[0], w_out[0])
        mid_act = pair_act + out_gate * out_fin[2]

        in_saved, in_left, in_right, in_gate = project_rows(mid_act, pair_mask, ln_pair[1], w_in[1])
        in_left_cols = lax.all_to_all(in_left, 'dap', 1, 0, tiled=True)
        in_right_all = lax.all_gather(in_right, 'dap', axis=0, tiled=True)
        in_tri = jnp.einsum('kic,kjc->ijc', in_left_cols, in_right_all, preferred_element_type=jnp.float32)
        in_fin = finish_rows(in_tri, ln_tri[1], w_out[1])

        d_in_tri, d_in_gate, gw_out_in, gln_tri_in = finish_back(in_fin, in_gate, grad_out, w_out[1])
        d_left_cols = jnp.einsum('ijc,kjc->kic', d_in_tri, in_right_all, preferred_element_type=jnp.float32).astype(jnp.bfloat16)
        d_in_left = lax.all_to_all(d_left_cols, 'dap', 0, 1, tiled=True)
        part_right_in = jnp.einsum('ijc,kic->kjc', d_in_tri, in_left_cols, preferred_element_type=jnp.float32)
        d_in_right = lax.psum_scatter(part_right_in, 'dap', scatter_dimension=0, tiled=True).astype(jnp.bfloat16)
        d_mid_ln, gln_pair_in, gw_in_in = project_back(in_saved, d_in_left, d_in_right, d_in_gate, w_in[1])
        d_mid = grad_out + d_mid_ln

        d_out_tri, d_out_gate, gw_out_out, gln_tri_out = finish_back(out_fin, out_gate, d_mid, w_out[0])
        d_out_left = jnp.einsum('ijc,jkc->ikc', d_out_tri, out_right_all, preferred_element_type=jnp.float32).astype(jnp.bfloat16)
        part_right_out = jnp.einsum('ijc,ikc->jkc', d_out_tri, out_left, preferred_element_type=jnp.float32)
        d_out_right = lax.psum_scatter(part_right_out, 'dap', scatter_dimension=0, tiled=True).astype(jnp.bfloat16)
        d_pair_ln, gln_pair_out, gw_in_out = project_back(out_saved, d_out_left, d_out_right, d_out_gate, w_in[0])

        weight_grads = lax.psum((jnp.stack([gln_pair_out, gln_pair_in]), jnp.stack([gw_in_out, gw_in_in]),
                                 jnp.stack([gln_tri_out, gln_tri_in]), jnp.stack([gw_out_out, gw_out_in])), 'dap')
        return (d_mid + d_pair_ln,) + tuple(weight_grads)

    return jax.shard_map(device_body, mesh=mesh,
                         in_specs=(row_spec, row_spec, row_spec, P(), P(), P(), P()),
                         out_specs=(row_spec, grad_spec, grad_spec, grad_spec, grad_spec),
                         check_vma=False)
```

profile of v0, /device:TPU:0, one launch (start us, length us, event | category | flops | bytes accessed | tf_op | source)
XLA Modules:
  0.0 3450.1 jit_solution(17057483282405285958)
XLA Ops:
  30.2 34.4 fusion.64
  64.6 28.4 multiply_convert_fusion.12
  106.2 286.9 %all-gather.3.cloned.1.call-done = bf16[512,512,128]{2,1,0:T(8,128)(2,1)} async-done(((bf16[64,512,128]{2,1,0:T(8,128)(2,1)}), bf16[512,512,128]{2,1,0:T(8,128)(2,1)}) %all-gather.3.cloned.1.call-update) | async-done | bytes 67108880 | tf_op jit(solution)/shard_map/all_gather | solution.py:69
  393.2 82.4 %copy.133 = bf16[512,512,128]{1,0,2:T(8,128)(2,1)} copy(bf16[512,512,128]{2,1,0:T(8,128)(2,1)} %all-gather.3.cloned.1.call-done) | data formatting | bytes 134217728 | tf_op jit(solution)/shard_map/all_gather | solution.py:69
  475.6 34.7 %bitcast_reduce_fusion.1 = (f32[64,512]{1,0:T(8,128)S(1)}, f32[128,512,64]{1,2,0:T(8,128)}) fusion(bf16[512,512,128]{1,0,2:T(8,128)(2,1)} %copy.133, bf16[64,512,128]{1,0,2:T(8,128)(2,1)} %copy.134), kind=kOutput, calls=%fused_computation.62 | convolution fusion | flops 4299128832 | bytes 92405760 | tf_op jit(solution)/shard_map/ikc,jkc->ijc/dot_general | solution.py:70
  529.4 28.5 fusion.84
  569.2 35.2 %fusion.61 = f32[64,512,640]{2,1,0:T(8,128)} fusion(bf16[2,128,640]{2,1,0:T(8,128)(2,1)S(1)} %copy-done.21, f32[64,512,128]{2,1,0:T(8,128)} %get-tuple-element.26, f32[128]{0:T(128)S(1)} %copy-done.45, f32[128]{0:T(128)S(1)} %copy-done.40, f32[64,512]{1,0:T(8,128)S(1)} %fusion.72, f32[64,512]{1,0:T(8,128)S(1)} %broadcast_multiply_fusion.1), kind=kOutput, calls=%fused_computation.125 | convolution fusion | flops 5389680640 | bytes 101090304 | tf_op jit(solution)/shard_map/ijc,cd->ijd/dot_general | solution.py:20
  604.4 41.2 %multiply_convert_fusion.9 = (bf16[64,512,128]{2,1,0:T(8,128)(2,1)}, bf16[64,512,128]{2,1,0:T(8,128)(2,1)}, bf16[64,512,128]{2,1,0:T(8,128)(2,1)}) fusion(f32[64,512,640]{2,1,0:T(8,128)} %fusion.61, f32[64,512]{1,0:T(8,128)S(1)} %convert_element_type.122, f32[64,512,128]{2,1,0:T(8,128)} %param.9), kind=kLoop, calls=%fused_computation.86 | loop fusion | flops 71303168 | bytes 125960192 | tf_op jit(solution)/shard_map/convert_element_type | solution.py:27
  657.8 185.4 %all_to_all.27 = bf16[64,512,128]{2,0,1:T(8,128)(2,1)} all-to-all(bf16[64,512,128]{2,0,1:T(8,128)(2,1)} %copy.138), channel_id=1, replica_groups=mesh['data'=1,'dap'=8] {'dap'}, dimensions={1} | all-to-all | bytes 16777216 | tf_op jit(solution)/shard_map/all_to_all | solution.py:75
  868.7 164.1 %all-gather.5.cloned.1.call-done = bf16[512,512,128]{2,1,0:T(8,128)(2,1)} async-done(((bf16[64,512,128]{2,1,0:T(8,128)(2,1)}), bf16[512,512,128]{2,1,0:T(8,128)(2,1)}) %all-gather.5.cloned.1.call-update) | async-done | bytes 67108880 | tf_op jit(solution)/shard_map/all_gather | solution.py:76
  1032.9 91.3 %copy.144 = bf16[512,512,128]{1,0,2:T(8,128)(2,1)} copy(bf16[512,512,128]{2,1,0:T(8,128)(2,1)} %all-gather.5.cloned.1.call-done) | data formatting | bytes 134217728 | tf_op jit(solution)/shard_map/all_gather | solution.py:76
  1124.2 32.1 fusion.86
  1201.2 21.1 fusion.12
  1255.9 51.7 %fusion.85 = f32[128,512,512]{2,1,0:T(8,128)} fusion(bf16[512,64,128]{0,1,2:T(8,128)(2,1)} %copy.142, bf16[64,512,128]{1,0,2:T(8,128)(2,1)} %copy.145), kind=kOutput, calls=%fused_computation.182 | convolution fusion | flops 4294967296 | bytes 150994944 | tf_op jit(solution)/shard_map/ijc,kic->kjc/dot_general | solution.py:83
  1307.6 133.1 %copy.150 = f32[128,512,512]{0,2,1:T(8,128)} copy(f32[128,512,512]{2,1,0:T(8,128)} %fusion.85) | data formatting | bytes 268435456 | tf_op jit(solution)/shard_map/ijc,kic->kjc/dot_general | solution.py:83
  1440.8 32.2 convert_bitcast_fusion.1
  1486.6 98.6 %all_to_all.28 = bf16[512,64,128]{2,1,0:T(8,128)(2,1)} all-to-all(bf16[512,64,128]{2,1,0:T(8,128)(2,1)} %copy.146), channel_id=1, replica_groups=mesh['data'=1,'dap'=8] {'dap'}, dimensions={0} | all-to-all | bytes 16777216 | tf_op jit(solution)/shard_map/all_to_all | solution.py:82
  1639.6 533.2 %reduce-scatter.3.cloned.1.call-done = f32[64,512,128]{2,1,0:T(8,128)} async-done(((f32[512,512,128]{2,1,0:T(8,128)}), f32[64,512,128]{2,1,0:T(8,128)}) %reduce-scatter.3.cloned.1.call-update) | async-done | bytes 16777232 | tf_op jit(solution)/shard_map/reduce_scatter | solution.py:84
  2226.9 23.8 fusion.10
  2250.8 23.3 fusion.13
  2274.1 23.7 multiply_convert_fusion.3
  2340.7 56.7 %fusion.55 = f32[128,512,512]{2,1,0:T(8,128)} fusion(bf16[64,512,128]{1,0,2:T(8,128)(2,1)} %copy.134, f32[64,512]{1,0:T(8,128)S(1)} %negate_multiply_fusion.1, bf16[64,512,128]{1,0,2:T(8,128)(2,1)} %copy.155, f32[128,512,64]{1,2,0:T(8,128)} %get-tuple-element.45, f32[64,512]{1,0:T(8,128)S(1)} %multiply_multiply_fusion.1, f32[128]{0:T(128)S(1)} %copy-done.37, ...), kind=kOutput, calls=%fused_computation.117 | convolution fusion | flops 4332716032 | bytes 168296960 | tf_op jit(solution)/shard_map/ijc,ikc->jkc/dot_general | solution.py:90
  2397.5 134.1 %copy.159 = f32[128,512,512]{0,1,2:T(8,128)} copy(f32[128,512,512]{2,1,0:T(8,128)} %fusion.55) | data formatting | bytes 268435456 | tf_op jit(solution)/shard_map/ijc,ikc->jkc/dot_general | solution.py:90
  2548.5 34.3 fusion.56
  2613.1 24.4 convolution_bitcast_fusion
  2667.7 595.9 %reduce-scatter.5.cloned.1.call-done = f32[64,512,128]{2,1,0:T(8,128)} async-done(((f32[512,512,128]{2,1,0:T(8,128)}), f32[64,512,128]{2,1,0:T(8,128)}) %reduce-scatter.5.cloned.1.call-update) | async-done | bytes 16777232 | tf_op jit(solution)/shard_map/reduce_scatter | solution.py:91
  3279.9 23.4 fusion.43
  3324.2 22.4 convolution_bitcast_fusion.1
  3346.6 23.8 fusion.8
  3370.4 22.6 fusion.15
  3394.0 23.2 add_add_fusion.4
  3417.2 22.4 all-reduce
  (225 shorter events, 466.4 us)
Async XLA Ops:
  7.2 386.0 %all-gather.3.cloned.1.call-start = ((), (), s32[]{:S(2)}) async-start(), calls=%async_computation.4 | async-start | bytes 75497472 | tf_op jit(solution)/shard_map/all_gather | solution.py:69
  8.5 21.1 copy-start.38
  8.5 21.1 copy-start.43
  9.4 594.9 %copy-start.8 = (f32[64,512]{1,0:T(8,128)}, f32[64,512]{1,0:T(8,128)S(1)}, u32[]{:S(2)}) copy-start(f32[64,512]{1,0:T(8,128)S(1)} %convert_element_type.122) | copy-start | bytes 393220
  93.0 939.9 %all-gather.5.cloned.1.call-start = ((), (), s32[]{:S(2)}) async-start(), calls=%async_computation.5 | async-start | bytes 75497472 | tf_op jit(solution)/shard_map/all_gather | solution.py:76
  106.2 412.1 %copy-start.36 = (f32[128]{0:T(128)}, f32[128]{0:T(128)S(1)}, u32[]{:S(2)}) copy-start(f32[128]{0:T(128)S(1)} %get-tuple-element.38) | copy-start | bytes 1540
  518.3 39.6 %copy-start.32 = (f32[64,512]{1,0:T(8,128)}, f32[64,512]{1,0:T(8,128)S(1)}, u32[]{:S(2)}) copy-start(f32[64,512]{1,0:T(8,128)S(1)} %multiply_reduce_fusion.2) | copy-start | bytes 393220
  557.9 46.4 %copy-start.13 = (f32[64,512]{1,0:T(8,128)}, f32[64,512]{1,0:T(8,128)S(1)}, u32[]{:S(2)}) copy-start(f32[64,512]{1,0:T(8,128)S(1)} %broadcast_multiply_fusion.1) | copy-start | bytes 393220
  569.1 35.3 %copy-start.34 = (f32[64,512]{1,0:T(8,128)}, f32[64,512]{1,0:T(8,128)S(1)}, u32[]{:S(2)}) copy-start(f32[64,512]{1,0:T(8,128)S(1)} %multiply_reduce_fusion.1) | copy-start | bytes 393220
  569.1 35.2 %copy-start.18 = (f32[64,512]{1,0:T(8,128)}, f32[64,512]{1,0:T(8,128)S(1)}, u32[]{:S(2)}) copy-start(f32[64,512]{1,0:T(8,128)S(1)} %fusion.72) | copy-start | bytes 393220
  645.6 1527.1 %reduce-scatter.3.cloned.1.call-start = ((), (), s32[]{:S(2)}) async-start(), calls=%async_computation.6 | async-start | bytes 150994944 | tf_op jit(solution)/shard_map/reduce_scatter | solution.py:84
  1183.7 38.7 %copy-start.24 = (f32[64,512]{1,0:T(8,128)}, f32[64,512]{1,0:T(8,128)S(1)}, u32[]{:S(2)}) copy-start(f32[64,512]{1,0:T(8,128)S(1)} %broadcast_multiply_fusion) | copy-start | bytes 393220
  1201.2 21.1 copy-start.27
  1440.8 1822.8 %reduce-scatter.5.cloned.1.call-start = ((), (), s32[]{:S(2)}) async-start(), calls=%async_computation.7 | async-start | bytes 150994944 | tf_op jit(solution)/shard_map/reduce_scatter | solution.py:91
  2172.8 38.4 %slice-start.4 = ((s8[16777216]{0:T(1024)(128)(4,1)}), s8[4194304]{0:T(1024)(128)(4,1)S(1)}, s32[]{:S(2)}) async-start(s8[16777216]{0:T(1024)(128)(4,1)} %bitcast.189), calls=%async_computation.13 | async-start | bytes 8388608
  2172.8 38.4 %slice-start.5 = ((s8[16777216]{0:T(1024)(128)(4,1)}), s8[4194304]{0:T(1024)(128)(4,1)S(1)}, s32[]{:S(2)}) async-start(s8[16777216]{0:T(1024)(128)(4,1)} %bitcast.189), calls=%async_computation.14 | async-start | bytes 8388608
  2226.9 23.9 copy-start.35
  2226.9 23.9 copy-start.19
  2250.7 23.4 slice-start.8
  2250.8 23.3 slice-start.9
  2531.6 908.0 %all-reduce.4.cloned.1.call-start = ((), (), s32[]{:S(2)}) async-start(), calls=%async_computation.8 | async-start | bytes 1572864 | tf_op jit(solution)/shard_map/psum | solution.py:94
  2596.7 40.8 %slice-start.10 = ((s8[8388608]{0:T(1024)(128)(4,1)}), s8[4194304]{0:T(1024)(128)(4,1)S(1)}, s32[]{:S(2)}) async-start(s8[8388608]{0:T(1024)(128)(4,1)} %bitcast.193), calls=%async_computation.19 | async-start | bytes 8388608
  2613.1 24.5 slice-start.11
  2613.1 24.5 copy-start.10
  3279.9 44.2 %slice-start = ((s8[16777216]{0:T(1024)(128)(4,1)}), s8[4194304]{0:T(1024)(128)(4,1)S(1)}, s32[]{:S(2)}) async-start(s8[16777216]{0:T(1024)(128)(4,1)} %bitcast.187), calls=%async_computation.9 | async-start | bytes 8388608
  3279.9 44.2 %slice-start.1 = ((s8[16777216]{0:T(1024)(128)(4,1)}), s8[4194304]{0:T(1024)(128)(4,1)S(1)}, s32[]{:S(2)}) async-start(s8[16777216]{0:T(1024)(128)(4,1)} %bitcast.187), calls=%async_computation.10 | async-start | bytes 8388608
  3279.9 44.2 %slice-start.2 = ((s8[16777216]{0:T(1024)(128)(4,1)}), s8[4194304]{0:T(1024)(128)(4,1)S(1)}, s32[]{:S(2)}) async-start(s8[16777216]{0:T(1024)(128)(4,1)} %bitcast.187), calls=%async_computation.11 | async-start | bytes 8388608
  3324.1 22.4 copy-start.23
  3346.6 23.8 copy-start.31
  3393.9 23.2 copy-start.56
  3394.0 23.2 copy-start.57
  3394.0 23.2 copy-start.50
  (48 other events, 640.6 us)
Sparse Core Ops, SparseCore 0:
  93.1 300.0 all-gather.2
  645.7 387.0 all-gather.4
  1440.9 731.8 reduce-scatter.2
  2531.7 731.8 reduce-scatter.4
  3394.1 44.3 all-reduce.3
where the time goes:
time: 3470 us; the launch traced here: 3450 us
  waiting for transfers between devices  1580 us (46%)
  local copies, waits for them, and re-layouts  594 us (17%)
  matrix products  503 us (14%)
  other arithmetic  451 us (13%)
  blocking collectives  306 us (9%)
    reduce_scatter x1, waiting for transfers between devices, device_body(): lax.psum_scatter(part_right_out, 'dap', scatter_dimension=0, tiled=True)  596 us
    reduce_scatter x1, waiting for transfers between devices, device_body(): lax.psum_scatter(part_right_in, 'dap', scatter_dimension=0, tiled=True)  533 us
    all_gather x1, waiting for transfers between devices, device_body(): out_right_all = lax.all_gather(out_right, 'dap', axis=0, tiled=True)  287 us
    all_to_all x1, blocking collectives, device_body(): in_left_cols = lax.all_to_all(in_left, 'dap', 1, 0, tiled=True)  185 us
    all_gather x1, waiting for transfers between devices, device_body(): in_right_all = lax.all_gather(in_right, 'dap', axis=0, tiled=True)  164 us
    dot_general x1, local copies, waits for them, and re-layouts, device_body(): jnp.einsum('ijc,ikc->jkc', d_out_tri, out_left, preferred_element_type=jn...  134 us
    dot_general x1, local copies, waits for them, and re-layouts, device_body(): jnp.einsum('ijc,kic->kjc', d_in_tri, in_left_cols, preferred_element_type...  133 us
    unnamed x10, other arithmetic  108 us
  transfers between devices with their start and end apart: 5, of which 4 were waited for; matrix products, arithmetic and copies ran while one was open for 9% of the time, Pallas kernels for 0%

commit v1 on v0

v1 whole, which is shorter than its diff:
```python
import functools

import jax
import jax.numpy as jnp
from jax import lax
from jax.experimental import pallas as pl
from jax.experimental.pallas import tpu as pltpu
from jax.sharding import PartitionSpec as P


LN_EPS = 1e-5
F32, BF16 = jnp.float32, jnp.bfloat16
N, ROWS, CH, HALF, TILE, DEV, BIG = 512, 64, 128, 64, 128, 8, 10**10
RB = 16
HR = 32
NCH = 4
STRIDE = 72
PAD = 24
VMEM = 62 * 1024 * 1024


def nn(a, b):
    return lax.dot_general(a, b, (((1,), (0,)), ((), ())), preferred_element_type=F32)


def nt(a, b):
    return lax.dot_general(a, b, (((1,), (1,)), ((), ())), preferred_element_type=F32)


def tn(a, b):
    return lax.dot_general(a, b, (((0,), (0,)), ((), ())), preferred_element_type=F32)


def sigmoid(v):
    return 0.5 * jnp.tanh(0.5 * v) + 0.5


def loop(count, body, unroll=1):
    def step(i, carry):
        body(i)
        return carry

    lax.fori_loop(0, count, step, 0, unroll=unroll)


def call(body, grid, in_specs, out_specs, out_shape, scratch=(), prefetch=0, aliases=None, flops=1000):
    return pl.pallas_call(
        body,
        grid_spec=pltpu.PrefetchScalarGridSpec(num_scalar_prefetch=prefetch, grid=grid, in_specs=in_specs,
                                               out_specs=out_specs, scratch_shapes=list(scratch)),
        out_shape=out_shape,
        input_output_aliases=aliases or {},
        compiler_params=pltpu.CompilerParams(dimension_semantics=("arbitrary",) * len(grid), vmem_limit_bytes=VMEM),
        cost_estimate=pl.CostEstimate(flops=flops, bytes_accessed=flops // 100, transcendentals=0))


def full(shape):
    return pl.BlockSpec(shape, lambda *_: (0,) * len(shape))


def sds(shape, dtype):
    return jax.ShapeDtypeStruct(shape, dtype)


def ln_rows(v, gain, bias):
    mean = jnp.mean(v, axis=-1, keepdims=True)
    cen = v - mean
    var = jnp.mean(cen * cen, axis=-1, keepdims=True)
    return cen * lax.rsqrt(var + LN_EPS) * gain + bias


def ln_kernel(z_ref, g_ref, *rest):
    o_ref, full_ref = rest[-2:]

    def row(r):
        v = ln_rows(z_ref[r], g_ref[0:1], g_ref[1:2]).astype(BF16)
        o_ref[r] = v
        full_ref[r] = v

    loop(RB, row)


def chained(in_specs, args, prev, first_out):
    if prev is None:
        return in_specs, args, {}
    aliases = {len(args) + i: first_out + i for i in range(len(prev))}
    return in_specs + [pl.BlockSpec(memory_space=pl.ANY)] * len(prev), args + list(prev), aliases


def ln_chunk(z, g, t, prev):
    zs = pl.BlockSpec((RB, N, CH), lambda i: (t, 0, 0))
    loc = pl.BlockSpec((RB, N, CH), lambda i: (0, 0, 0))
    in_specs, args, aliases = chained([zs, full((2, CH))], [z, g], prev, 1)
    return call(ln_kernel, (1,), in_specs, [loc, zs], [sds((RB, N, CH), BF16), sds((ROWS, N, CH), BF16)],
                aliases=aliases, flops=BIG)(*args)


def proj_kernel(count, id_ref, *refs):
    z_refs, (m_ref, w_ref) = refs[:count], refs[count:count + 2]
    a_ref, b_ref, sa, sb, buf, sem = refs[-6:]
    step = pl.program_id(0)
    slot = lax.rem(step, 2)

    def copy(j):
        return pltpu.make_async_copy(z_refs[j], buf.at[j % 2], sem.at[j % 2])

    for j in range(count):
        @pl.when(step == j)
        def _():
            if j == 0:
                copy(j).start()
            if j + 1 < count:
                copy(j + 1).start()
            copy(j).wait()

    def row(r):
        base = pl.multiple_of(r * STRIDE, 8)
        for l in range(2):
            p = nt(w_ref[...], buf[slot, r, l * 256:(l + 1) * 256, :])
            m = m_ref[pl.ds(r, 1), l * 256:(l + 1) * 256]
            av = m * sigmoid(p[HALF:TILE]) * p[:HALF]
            bv = m * sigmoid(p[TILE + HALF:]) * p[TILE:TILE + HALF]
            for t in range(2):
                sa[2 * l + t, pl.ds(base, HALF), :] = av[:, t * TILE:(t + 1) * TILE]
                sb[2 * l + t, pl.ds(base, HALF), :] = bv[:, t * TILE:(t + 1) * TILE]

    loop(RB, row)

    def chan(c):
        for l in range(4):
            a_ref[c, :, l * TILE:(l + 1) * TILE] = sa[l, pl.ds(c, RB, stride=STRIDE), :].astype(BF16)
            b_ref[c, :, l * TILE:(l + 1) * TILE] = sb[l, pl.ds(c, RB, stride=STRIDE), :].astype(BF16)

    loop(HALF, chan, 2)


def proj_chunk(ids, first, blocks, mask, w, t, prev):
    count = len(blocks)

    def place(i, s):
        return ((s[0] * 2 + s[1]) ^ (first + i)) * NCH + t

    out = pl.BlockSpec((HALF, RB, N), lambda i, s: (0, place(i, s), 0))
    in_specs, args, aliases = chained(
        [pl.BlockSpec(memory_space=pl.ANY)] * count + [pl.BlockSpec((RB, N), lambda i, s: (place(i, s), 0)),
                                                       full((256, CH))], [*blocks, mask, w], prev, 0)
    return call(functools.partial(proj_kernel, count), (count,), in_specs, [out, out], [sds((HALF, N, N), BF16)] * 2,
                [pltpu.VMEM((4, RB * STRIDE, TILE), F32)] * 2
                + [pltpu.VMEM((2, RB, N, CH), BF16), pltpu.SemaphoreType.DMA((2,))], prefetch=1,
                aliases={k + 1: v for k, v in aliases.items()}, flops=BIG)(ids, *args)


CB = 8


def swap_out(h, v, keep_ref, send_ref, c):
    lo, hi = v[:ROWS].astype(keep_ref.dtype), v[ROWS:].astype(keep_ref.dtype)
    keep_ref[c] = jnp.where(h == 0, lo, hi)
    send_ref[c] = jnp.where(h == 0, hi, lo)


def tri_kernel(form, id_ref, a_ref, b_ref, keep_ref, send_ref):
    h = id_ref[1]

    def chan(c):
        v = nt(a_ref[c], b_ref[c]) if form == 'out' else tn(a_ref[c], b_ref[c])
        lo, hi = v[:ROWS], v[ROWS:]
        keep, send = jnp.where(h == 0, lo, hi), jnp.where(h == 0, hi, lo)
        for l in range(4):
            keep_ref[l, c] = keep[:, l * TILE:(l + 1) * TILE]
            send_ref[l, c] = send[:, l * TILE:(l + 1) * TILE]

    loop(CB, chan)


def tri_forward(form, ids, a, b):
    if form == 'out':
        a_spec = pl.BlockSpec((CB, TILE, N), lambda c, s: (c, s[0], 0))
    else:
        a_spec = pl.BlockSpec((CB, N, TILE), lambda c, s: (c, 0, s[0]))
    half = pl.BlockSpec((4, CB, ROWS, TILE), lambda c, s: (0, c, 0, 0))
    return call(functools.partial(tri_kernel, form), (HALF // CB,),
                [a_spec, pl.BlockSpec((CB, N, N), lambda c, s: (c, 0, 0))], [half, half],
                [sds((4, HALF, ROWS, TILE), F32)] * 2, prefetch=1, flops=BIG)(ids, a, b)


def row_ds(start, size):
    return pl.ds(pl.multiple_of(start, size), size)


def fill_dx(h, halves, c, dx):
    for e in range(2):
        for o in range(2):
            dx[row_ds((h ^ o) * ROWS + e * HR, HR), :] = halves[2 * e + o][c]


def da_out_kernel(id_ref, b_ref, *rest):
    halves, (keep_ref, send_ref, dx) = rest[:4], rest[-3:]
    h = id_ref[1]

    def chan(c):
        fill_dx(h, halves, c, dx)
        swap_out(h, nn(dx[...], b_ref[c]), keep_ref, send_ref, c)

    loop(CB, chan)


def da_in_kernel(id_ref, b_ref, *rest):
    halves, outs, (dx, res) = rest[:4], rest[-10:-2], rest[-2:]
    idx = id_ref[0] * 2 + id_ref[1]

    def chan(c):
        fill_dx(id_ref[1], halves, c, dx)
        res[...] = nt(b_ref[c].reshape(DEV * HR, N), dx[...]).astype(BF16)
        for s in range(DEV):
            outs[s][c] = res[row_ds((idx ^ s) * HR, HR), :]

    loop(CB, chan)


def fill_pieces(idx, pieces, c, dx):
    for e in range(2):
        for s in range(DEV):
            dx[row_ds((idx ^ s) * ROWS + e * HR, HR), :] = pieces[e * DEV + s][c]


def db_out_kernel(id_ref, a_ref, *rest):
    pieces, (keep_ref, send_ref, dx) = rest[:2 * DEV], rest[-3:]

    def chan(c):
        fill_pieces(id_ref[0] * 2 + id_ref[1], pieces, c, dx)
        swap_out(id_ref[1], tn(dx[...], a_ref[c]), keep_ref, send_ref, c)

    loop(CB, chan)


def db_in_kernel(id_ref, a_ref, *rest):
    pieces, outs, (dx, res) = rest[:2 * DEV], rest[-10:-2], rest[-2:]
    idx = id_ref[0] * 2 + id_ref[1]

    def chan(c):
        fill_pieces(idx, pieces, c, dx)
        res[...] = nn(a_ref[c].reshape(DEV * HR, N), dx[...]).astype(BF16)
        for s in range(DEV):
            outs[s][c] = res[row_ds((idx ^ s) * HR, HR), :]

    loop(CB, chan)


def tri_back(kind, ids, mat, parts, half=None, after=()):
    rows = pl.BlockSpec((CB, HR, parts[0].shape[2]), lambda c, s: (c, 0, 0))
    dx = pltpu.VMEM((TILE, N) if kind.startswith('da') else (N, TILE), BF16)
    tail = [pl.BlockSpec(memory_space=pl.ANY)] * len(after)
    bodies = {'da_out': da_out_kernel, 'db_out': db_out_kernel, 'da_in': da_in_kernel, 'db_in': db_in_kernel}
    if half is None:
        keep = pl.BlockSpec((CB, ROWS, N), lambda c, s: (c, 0, 0))
        return call(bodies[kind], (HALF // CB,),
                    [pl.BlockSpec((CB, N, N), lambda c, s: (c, 0, 0))] + [rows] * len(parts) + tail, [keep, keep],
                    [sds((HALF, ROWS, N), BF16)] * 2, [dx], prefetch=1, flops=BIG)(ids, mat, *parts, *after)
    piece = pl.BlockSpec((CB, HR, TILE), lambda c, s: (c, 0, 0))
    return call(bodies[kind], (HALF // CB,),
                [pl.BlockSpec((CB, DEV, HR, N), lambda c, s: (c, 0, half, 0))] + [rows] * len(parts) + tail,
                [piece] * DEV, [sds((HALF, HR, TILE), BF16)] * DEV, [dx, pltpu.VMEM((DEV * HR, TILE), BF16)],
                prefetch=1, flops=BIG)(ids, mat.reshape(HALF, DEV, ROWS, N), *parts, *after)


def x_row(xk_ref, xr_ref, r, rb):
    halves = []
    for ref in (xk_ref, xr_ref):
        flat = ref.reshape(4, HALF * rb, TILE)
        halves.append(jnp.concatenate([flat[l, pl.ds(r, HALF, stride=rb), :] for l in range(4)], axis=1))
    return jnp.concatenate(halves, axis=0)


def x_norm(x):
    mean = jnp.mean(x, axis=0, keepdims=True)
    cen = x - mean
    rstd = lax.rsqrt(jnp.mean(cen * cen, axis=0, keepdims=True) + LN_EPS)
    return cen * rstd, rstd


def fin_kernel(xk_ref, xr_ref, z_ref, zn_ref, wg_ref, wo_ref, gt_ref, g1_ref, *rest):
    loc_ref, z1_ref, zn1_ref = rest[-3:]

    def row(r):
        xhat, _ = x_norm(x_row(xk_ref, xr_ref, r, RB))
        xn = (xhat * gt_ref[:, 0:1] + gt_ref[:, 1:2]).astype(BF16)
        gate = sigmoid(nn(zn_ref[r], wg_ref[...]))
        z1 = z_ref[r] + gate * tn(xn, wo_ref[...])
        z1_ref[r] = z1
        zn1 = ln_rows(z1, g1_ref[0:1], g1_ref[1:2]).astype(BF16)
        loc_ref[r] = zn1
        zn1_ref[r] = zn1

    loop(RB, row)


def fin_chunk(xk, xr, z, zn, wg, wo, gt, g1, t, prev):
    xs = pl.BlockSpec((4, HALF, RB, TILE), lambda i: (0, 0, t, 0))
    zs = pl.BlockSpec((RB, N, CH), lambda i: (t, 0, 0))
    loc = pl.BlockSpec((RB, N, CH), lambda i: (0, 0, 0))
    in_specs, args, aliases = chained([xs, xs, zs, zs, full((CH, CH)), full((CH, CH)), full((CH, 2)), full((2, CH))],
                                      [xk, xr, z, zn, wg, wo, gt, g1], prev, 1)
    return call(fin_kernel, (1,), in_specs, [loc, zs, zs],
                [sds((RB, N, CH), BF16), sds((ROWS, N, CH), F32), sds((ROWS, N, CH), BF16)],
                aliases=aliases, flops=BIG)(*args)


def finb_kernel(id_ref, xk_ref, xr_ref, zn_ref, dz_ref, wg_ref, wo_ref, gt_ref, *rest):
    dg_ref, dk_ref, ds_ref = rest[-15:-12]
    pieces, (dwo_ref, dga_ref, dbi_ref, sd) = rest[-12:-4], rest[-4:]

    @pl.when(pl.program_id(0) == 0)
    def _():
        dwo_ref[...] = jnp.zeros_like(dwo_ref)
        dga_ref[...] = jnp.zeros_like(dga_ref)
        dbi_ref[...] = jnp.zeros_like(dbi_ref)

    def row(r):
        base = pl.multiple_of(r * STRIDE, 8)
        xhat, rstd = x_norm(x_row(xk_ref, xr_ref, r, RB))
        gain = gt_ref[:, 0:1]
        xn = (xhat * gain + gt_ref[:, 1:2]).astype(BF16)
        gate = sigmoid(nn(zn_ref[r], wg_ref[...]))
        proj = tn(xn, wo_ref[...])
        dz = dz_ref[r]
        gated = dz * gate
        dg_ref[r] = (gated * proj * (1.0 - gate)).astype(BF16)
        dproj = gated.astype(BF16)
        dwo_ref[...] += nn(xn, dproj)
        dn = nt(wo_ref[...], dproj).astype(BF16).astype(F32)
        prod = dn * xhat
        dga, dbi = dga_ref[...], dbi_ref[...]
        for l in range(4):
            dga += prod[:, l * TILE:(l + 1) * TILE]
            dbi += dn[:, l * TILE:(l + 1) * TILE]
        dga_ref[...] = dga
        dbi_ref[...] = dbi
        dxh = dn * gain
        m1 = jnp.mean(dxh, axis=0, keepdims=True)
        m2 = jnp.mean(dxh * xhat, axis=0, keepdims=True)
        dx = rstd * (dxh - m1 - xhat * m2)
        for e in range(2):
            for l in range(4):
                sd[e, l, pl.ds(base, HALF), :] = dx[e * HALF:(e + 1) * HALF, l * TILE:(l + 1) * TILE]

    loop(RB, row, 2)
    q = id_ref[0]

    def chan(c):
        for l in range(4):
            dk_ref[c, :, l * TILE:(l + 1) * TILE] = sd[0, l, pl.ds(c, RB, stride=STRIDE), :].astype(BF16)
            ds_ref[c, :, l * TILE:(l + 1) * TILE] = sd[1, l, pl.ds(c, RB, stride=STRIDE), :].astype(BF16)
        for s in range(DEV):
            pieces[s][c] = sd[s & 1, q ^ (s >> 1), pl.ds(c, RB, stride=STRIDE), :].astype(BF16)

    loop(HALF, chan, 2)


def part_spec(v, e):
    off = e * (HR // RB) if v.shape[0] == ROWS else 0
    return pl.BlockSpec((RB,) + v.shape[1:], lambda i, s: (off + i,) + (0,) * (v.ndim - 1))


def fin_back(e, ids, xk, xr, zn, dz, wg, wo, gt, after=()):
    x4 = pl.BlockSpec((4, HALF, RB, TILE), lambda i, s: (0, 0, e * (HR // RB) + i, 0))
    xs = pl.BlockSpec((HALF, RB, N), lambda i, s: (0, i, 0))
    ps = pl.BlockSpec((HALF, RB, TILE), lambda i, s: (0, i, 0))
    dgs = pl.BlockSpec((RB, N, CH), lambda i, s: (i, 0, 0))
    acc = full((CH, CH))
    return call(finb_kernel, (HR // RB,), [x4, x4, part_spec(zn, e), part_spec(dz, e), acc, acc, full((CH, 2))]
                + [pl.BlockSpec(memory_space=pl.ANY)] * len(after),
                [dgs, xs, xs] + [ps] * DEV + [acc] * 3,
                [sds((HR, N, CH), BF16)] + [sds((HALF, HR, N), BF16)] * 2 + [sds((HALF, HR, TILE), BF16)] * DEV
                + [sds((CH, CH), F32)] * 3,
                [pltpu.VMEM((2, 4, RB * STRIDE, TILE), F32)], prefetch=1, flops=BIG)(
                    ids, xk, xr, zn, dz, wg, wo, gt, *after)


def projb_kernel(form, id_ref, *refs):
    n = 2 if form == 'out' else 8
    da, db = refs[:n], refs[n:2 * n]
    zn_ref, z_ref, dz_ref, dg_ref, m_ref, w_ref, wg_ref, g_ref = refs[2 * n:2 * n + DEV]
    o_ref, dw_ref, dwg_ref, dga_ref, dbi_ref, sa, sb = refs[-7:]
    q = id_ref[0]

    @pl.when(pl.program_id(0) == 0)
    def _():
        for ref in (dw_ref, dwg_ref, dga_ref, dbi_ref):
            ref[...] = jnp.zeros_like(ref)

    def chan(c):
        base = pl.multiple_of(c * PAD, 8)
        for src, dst in ((da, sa), (db, sb)):
            for s in range(n):
                if form == 'out':
                    for l in range(4):
                        dst[s, l, pl.ds(base, RB), :] = src[s][c, :, l * TILE:(l + 1) * TILE].astype(F32)
                else:
                    dst[s & 1, q ^ (s >> 1), pl.ds(base, RB), :] = src[s][c].astype(F32)

    loop(HALF, chan, 2)

    def row(r):
        zn = zn_ref[r]
        m = m_ref[pl.ds(r, 1), :]
        dg = dg_ref[r]
        dzn = nt(dg, wg_ref[...])
        dwg_ref[...] += tn(zn, dg)
        for e in range(2):
            w = w_ref[e * 256:(e + 1) * 256, :]
            p = nt(w, zn)
            parts = []
            for k, src in enumerate((sa, sb)):
                d = jnp.concatenate([src[e, l, pl.ds(r, HALF, stride=PAD), :] for l in range(4)], axis=1) * m
                lin = p[k * TILE:k * TILE + 64]
                sig = sigmoid(p[k * TILE + 64:k * TILE + TILE])
                ds = d * sig
                parts += [ds.astype(BF16), (ds * lin * (1.0 - sig)).astype(BF16)]
            cat = jnp.concatenate(parts, axis=0)
            dzn += tn(cat, w)
            dw_ref[e * 256:(e + 1) * 256, :] += nn(cat, zn)
        dn = dzn.astype(BF16).astype(F32)
        z = z_ref[r]
        mean = jnp.mean(z, axis=-1, keepdims=True)
        cen = z - mean
        rstd = lax.rsqrt(jnp.mean(cen * cen, axis=-1, keepdims=True) + LN_EPS)
        zhat = cen * rstd
        dga_ref[...] += jnp.sum((dn * zhat).reshape(N // 8, 8, CH), axis=0)
        dbi_ref[...] += jnp.sum(dn.reshape(N // 8, 8, CH), axis=0)
        dh = dn * g_ref[0:1]
        m1 = jnp.mean(dh, axis=-1, keepdims=True)
        m2 = jnp.mean(dh * zhat, axis=-1, keepdims=True)
        o_ref[r] = dz_ref[r] + rstd * (dh - m1 - zhat * m2)

    loop(RB, row, 2)


def proj_back(form, e, ids, da, db, zn, z, dz, dg, mask, w, wg, g, prev=None, after=()):
    off = e * (HR // RB)
    if form == 'out':
        ps = pl.BlockSpec((HALF, RB, N), lambda i, s: (0, off + i, 0))
        o_spec, o_rows = part_spec(z, e), ROWS
    else:
        ps = pl.BlockSpec((HALF, RB, TILE), lambda i, s: (0, i, 0))
        o_spec, o_rows = pl.BlockSpec((RB, N, CH), lambda i, s: (i, 0, 0)), HR
    rows = [zn, z, dz, dg, mask]
    in_specs, args, aliases = chained(
        [ps] * (2 * len(da)) + [part_spec(v, e) for v in rows] + [full((512, CH)), full((CH, CH)), full((2, CH))],
        [*da, *db, *rows, w, wg, g], prev, 0)
    return call(functools.partial(projb_kernel, form), (HR // RB,),
                in_specs + [pl.BlockSpec(memory_space=pl.ANY)] * len(after),
                [o_spec, full((512, CH)), full((CH, CH)), full((DEV, CH)), full((DEV, CH))],
                [sds((o_rows, N, CH), F32), sds((512, CH), F32), sds((CH, CH), F32), sds((DEV, CH), F32),
                 sds((DEV, CH), F32)],
                [pltpu.VMEM((2, 4, HALF * PAD, TILE), F32)] * 2, prefetch=1,
                aliases={k + 1: v for k, v in aliases.items()}, flops=2 * BIG)(
                    ids, *args, *after)


def solution(mesh):
    row_spec = P(('data', 'dap'))
    grad_spec = P('data')

    def xor(v, s):
        if s == 0:
            return v
        return lax.ppermute(v, 'dap', [(i, i ^ s) for i in range(DEV)])

    def device_body(pair_act, pair_mask, grad_out, ln_pair, w_in, ln_tri, w_out):
        idx = lax.axis_index('dap').astype(jnp.int32)
        h = lax.rem(idx, 2)
        ids = jnp.stack([idx // 2, h])
        mask = pair_mask.astype(F32)
        mask_all = lax.all_gather(mask, 'dap', axis=0, tiled=True)
        g_pair = ln_pair.astype(F32)
        g_tri = ln_tri.astype(F32)

        def rel(v, axis):
            lo, hi = jnp.split(v, 2, axis=axis)
            return jnp.where(h == 0, v, jnp.concatenate([hi, lo], axis=axis))

        w_rel, wg, wo_rel, gt_rel = [], [], [], []
        for u in range(2):
            wt = w_in[u, :, :512].T.reshape(4, 2, HALF, CH).transpose(1, 0, 2, 3).reshape(512, CH)
            w_rel.append(rel(wt, 0))
            wg.append(w_in[u, :, 512:])
            wo_rel.append(rel(w_out[u], 0))
            gt_rel.append(rel(g_tri[u].T, 0))

        def spread(v):
            return [v] + [xor(v, s) for s in (1, 2, 4)]

        def gather_proj(parts, u):
            w, prev = w_rel[u][:256], None
            for t, (own, r1, _, _) in enumerate(parts):
                prev = proj_chunk(ids, 0, [own, r1], mask_all, w, t, prev)
            far = []
            for t, (_, _, r2, r4) in enumerate(parts):
                far.append(xor(r4, 2) if t % 2 else xor(r2, 4))
                near = [r2, xor(r2, 1), r4, xor(r4, 1)]
                prev = proj_chunk(ids, 2, near, mask_all, w, t, prev)
            for t, r6 in enumerate(far):
                r7 = xor(r6, 1)
                prev = proj_chunk(ids, 6, [r6, r7], mask_all, w, t, prev)
            return prev

        parts, prev = [], None
        for t in range(NCH):
            chunk, zn0 = ln_chunk(pair_act, g_pair[0], t, prev)
            parts, prev = parts + [spread(chunk)], [zn0]
        a0, b0 = gather_proj(parts, 0)
        x0k, x0s = tri_forward('out', ids, a0, b0)
        x0r = xor(x0s, 1)
        parts, prev = [], None
        for t in range(NCH):
            chunk, z1, zn1 = fin_chunk(x0k, x0r, pair_act, zn0, wg[0], wo_rel[0], gt_rel[0], g_pair[1], t, prev)
            parts, prev = parts + [spread(chunk)], [z1, zn1]
        a1, b1 = gather_proj(parts, 1)
        x1k, x1s = tri_forward('in', ids, a1, b1)
        x1r = xor(x1s, 1)

        def exchange(pieces):
            return [xor(v, s) for s, v in enumerate(pieces)]

        def split(out):
            dg, dk, ds = out[:3]
            return dg, [dk, xor(ds, 1)], exchange(out[3:11]), out[11:], dk

        fb1 = [split(fin_back(0, ids, x1k, x1r, zn1, grad_out, wg[1], wo_rel[1], gt_rel[1]))]
        out = fin_back(1, ids, x1k, x1r, zn1, grad_out, wg[1], wo_rel[1], gt_rel[1], (fb1[0][4],))
        fb1 += [split(out)]
        dx1, dp1 = fb1[0][1] + fb1[1][1], fb1[0][2] + fb1[1][2]
        da, db, last = [], [], fb1[1][4]
        for e in range(2):
            out = tri_back('da_in', ids, b1, dx1, e, (last,))
            da.append(exchange(out))
            out = tri_back('db_in', ids, a1, dp1, e, (out[0],))
            db.append(exchange(out))
            last = out[0]
        pb1, fb0 = [], []
        for e in range(2):
            pb1.append(proj_back('in', e, ids, da[e], db[e], zn1, z1, grad_out, fb1[e][0], mask, w_rel[1], wg[1],
                                 g_pair[1], after=(last,)))
            fb0.append(split(fin_back(e, ids, x0k, x0r, zn0, pb1[e][0], wg[0], wo_rel[0], gt_rel[0])))
            last = fb0[e][4]
        da_k, da_s = tri_back('da_out', ids, b0, fb0[0][1] + fb0[1][1])
        da_0 = [da_k, xor(da_s, 1)]
        db_k, db_s = tri_back('db_out', ids, a0, fb0[0][2] + fb0[1][2], after=(da_k,))
        db_0 = [db_k, xor(db_s, 1)]
        pb0, prev = [], None
        for e in range(2):
            pb0.append(proj_back('out', e, ids, da_0, db_0, zn0, pair_act, pb1[e][0], fb0[e][0], mask, w_rel[0], wg[0],
                                 g_pair[0], prev=prev))
            prev = [pb0[e][0]]

        def pack(fb, pb):
            dwo, dga, dbi = [fb[0][3][i] + fb[1][3][i] for i in range(3)]
            dw, dwg, dgp, dbp = [pb[0][i] + pb[1][i] for i in range(1, 5)]
            dw = rel(dw, 0).reshape(2, 4, HALF, CH).transpose(1, 0, 2, 3).reshape(512, CH)
            tri = jnp.stack([jnp.sum(rel(dga, 0), 1), jnp.sum(rel(dbi, 0), 1)])
            return lax.psum(jnp.concatenate([dw, dwg, rel(dwo, 0), dgp, dbp, tri], axis=0), 'dap')

        def unpack(v):
            dw, dwg, dwo, dgp, dbp, tri = jnp.split(v, [512, 640, 768, 776, 784])
            return (jnp.stack([jnp.sum(dgp, 0), jnp.sum(dbp, 0)]), jnp.concatenate([dw.T, dwg], axis=1), tri, dwo)

        packed = [pack(fb0, pb0), pack(fb1, pb1)]
        return (pb0[1][0],) + tuple(jnp.stack(v) for v in zip(*[unpack(v) for v in packed]))


    return jax.shard_map(device_body, mesh=mesh,
                         in_specs=(row_spec, row_spec, row_spec, P(), P(), P(), P()),
                         out_specs=(row_spec, grad_spec, grad_spec, grad_spec, grad_spec),
                         check_vma=False)
```

time: 3470 us -> 1780 us (0.51)
  Pallas kernels: 0 us -> 980 us
  waiting for transfers between devices: 1580 us -> 666 us
  local copies, waits for them, and re-layouts: 594 us -> 19.9 us
  matrix products: 503 us -> 0 us
  other arithmetic: 451 us -> 10.3 us
  blocking collectives: 306 us -> 0 us
  starting transfers between devices: 0.42 us -> 89.9 us
    reduce_scatter x2 -> x0, waiting for transfers between devices: 1130 us -> none  [the longest x1 596 us: device_body(): lax.psum_scatter(part_right_out, 'dap', scatter_dimension=0, tiled=True)]
    pallas_call x0 -> x48, Pallas kernels: none -> 980 us  [the longest x24 427 us: proj_chunk(): call(functools.partial(proj_kernel, count), (count,), in_specs, [out, out...]
    ppermute x0 -> x120, waiting for transfers between devices: none -> 621 us  [xor(): return lax.ppermute(v, 'dap', [(i, i ^ s) for i in range(DEV)])]
    dot_general x18 -> x0, matrix products: 503 us -> none  [the longest x2 69.6 us: project_rows(): jnp.einsum('ijc,cd->ijd', normed, w_in, preferred_element_type=jnp.float32)]
    all_gather x2 -> x1, waiting for transfers between devices: 451 us -> 0.01 us  [device_body(): mask_all = lax.all_gather(mask, 'dap', axis=0, tiled=True)]
    dot_general x5 -> x0, local copies, waits for them, and re-layouts: 311 us -> none  [the longest x1 134 us: device_body(): jnp.einsum('ijc,ikc->jkc', d_out_tri, out_left, preferred_element_type=jn...]
    all_to_all x2 -> x0, blocking collectives: 284 us -> none  [the longest x1 185 us: device_body(): in_left_cols = lax.all_to_all(in_left, 'dap', 1, 0, tiled=True)]
    all_gather x2 -> x0, local copies, waits for them, and re-layouts: 174 us -> none  [the longest x1 91.3 us: device_body(): in_right_all = lax.all_gather(in_right, 'dap', axis=0, tiled=True)]
  transfers between devices with their start and end apart: 5 -> 122, of which waited for: 4 -> 41; matrix products, arithmetic and copies ran while one was open for 9% -> 0% of each run, Pallas kernels for 0% -> 35%
where the time goes in v1:
time: 1780 us
  Pallas kernels  980 us (55%)
  waiting for transfers between devices  666 us (37%)
  starting transfers between devices  89.9 us (5%)
  local copies, waits for them, and re-layouts  19.9 us (1%)
    ppermute x120, waiting for transfers between devices, xor(): return lax.ppermute(v, 'dap', [(i, i ^ s) for i in range(DEV)])  621 us
    pallas_call x24, Pallas kernels, proj_chunk(): call(functools.partial(proj_kernel, count), (count,), in_specs, [out, out...  427 us
    pallas_call x4, Pallas kernels, proj_back(): call(functools.partial(projb_kernel, form), (HR // RB,), in_specs + [pl.B...  164 us
    pallas_call x4, Pallas kernels, fin_back(): call(finb_kernel, (HR // RB,), [x4, x4, part_spec(zn, e), part_spec(dz, e...  110 us
    ppermute x120, starting transfers between devices, xor(): return lax.ppermute(v, 'dap', [(i, i ^ s) for i in range(DEV)])  89.8 us
    pallas_call x4, Pallas kernels, tri_back(): call(bodies[kind], (HALF // CB,), [pl.BlockSpec((CB, DEV, HR, N), lambda...  78.4 us
    pallas_call x4, Pallas kernels, fin_chunk(): call(fin_kernel, (1,), in_specs, [loc, zs, zs], [sds((RB, N, CH), BF16),...  67.9 us
    pallas_call x2, Pallas kernels, tri_forward(): call(functools.partial(tri_kernel, form), (HALF // CB,), [a_spec, pl.Bloc...  54.1 us
  transfers between devices with their start and end apart: 122, of which 41 were waited for; matrix products, arithmetic and copies ran while one was open for 0% of the time, Pallas kernels for 35%

profile of v1, /device:TPU:0, one launch (start us, length us, event | category | flops | bytes accessed | tf_op | source)
XLA Modules:
  0.0 1781.3 jit_solution(13319639405926427869)
XLA Ops:
  48.8 42.7 %collective-permute-done.9.refs_0_ = bf16[16,512,128]{2,1,0:T(8,128)(2,1)} collective-permute-done((bf16[16,512,128]{2,1,0:T(8,128)(2,1)}, bf16[16,512,128]{2,1,0:T(8,128)(2,1)}, u32[]{:S(2)}, u32[]{:S(2)}) %collective-permute-start.9) | collective-permute-done | bytes 2097184 | tf_op jit(solution)/shard_map/ppermute | solution.py:468
  95.7 46.9 %collective-permute-done.6.refs_2_ = bf16[16,512,128]{2,1,0:T(8,128)(2,1)} collective-permute-done((bf16[16,512,128]{2,1,0:T(8,128)(2,1)}, bf16[16,512,128]{2,1,0:T(8,128)(2,1)}, u32[]{:S(2)}, u32[]{:S(2)}) %collective-permute-start.6) | collective-permute-done | bytes 2097184 | tf_op jit(solution)/shard_map/ppermute | solution.py:468
  142.7 42.8 %collective-permute-done.3.refs_0_ = bf16[16,512,128]{2,1,0:T(8,128)(2,1)} collective-permute-done((bf16[16,512,128]{2,1,0:T(8,128)(2,1)}, bf16[16,512,128]{2,1,0:T(8,128)(2,1)}, u32[]{:S(2)}, u32[]{:S(2)}) %collective-permute-start.3) | collective-permute-done | bytes 2097184 | tf_op jit(solution)/shard_map/ppermute | solution.py:468
  189.5 41.8 %collective-permute-done.refs_2_ = bf16[16,512,128]{2,1,0:T(8,128)(2,1)} collective-permute-done((bf16[16,512,128]{2,1,0:T(8,128)(2,1)}, bf16[16,512,128]{2,1,0:T(8,128)(2,1)}, u32[]{:S(2)}, u32[]{:S(2)}) %collective-permute-start) | collective-permute-done | bytes 2097184 | tf_op jit(solution)/shard_map/ppermute | solution.py:468
  294.2 24.5 %shard_map.118 = (bf16[64,512,512]{2,1,0:T(8,128)(2,1)}, bf16[64,512,512]{2,1,0:T(8,128)(2,1)}) custom-call(s32[2]{0:T(128)} %pad_add_fusion.id_ref, bf16[16,512,128]{2,1,0:T(8,128)(2,1)} %collective-permute-done.9.refs_0_, bf16[16,512,128]{2,1,0:T(8,128)(2,1)} %collective-permute-done.21.refs_1_, ...), custom_call_target="tpu_custom_call", output_to_operand_aliasing={{0}: (7, {}), {1}: (8, {})} | custom-call | flops 10000000000 | bytes 100000000 | tf_op jit(solution)/shard_map/pallas_call | solution.py:147
  319.3 24.5 %shard_map.119 = (bf16[64,512,512]{2,1,0:T(8,128)(2,1)}, bf16[64,512,512]{2,1,0:T(8,128)(2,1)}) custom-call(s32[2]{0:T(128)} %pad_add_fusion.id_ref, bf16[16,512,128]{2,1,0:T(8,128)(2,1)} %collective-permute-done.18.refs_0_, bf16[16,512,128]{2,1,0:T(8,128)(2,1)} %collective-permute-done.19.refs_1_, ...), custom_call_target="tpu_custom_call", output_to_operand_aliasing={{0}: (7, {}), {1}: (8, {})} | custom-call | flops 10000000000 | bytes 100000000 | tf_op jit(solution)/shard_map/pallas_call | solution.py:147
  343.8 24.4 %shard_map.120 = (bf16[64,512,512]{2,1,0:T(8,128)(2,1)}, bf16[64,512,512]{2,1,0:T(8,128)(2,1)}) custom-call(s32[2]{0:T(128)} %pad_add_fusion.id_ref, bf16[16,512,128]{2,1,0:T(8,128)(2,1)} %collective-permute-done.3.refs_0_, bf16[16,512,128]{2,1,0:T(8,128)(2,1)} %collective-permute-done.15.refs_1_, ...), custom_call_target="tpu_custom_call", output_to_operand_aliasing={{0}: (7, {}), {1}: (8, {})} | custom-call | flops 10000000000 | bytes 100000000 | tf_op jit(solution)/shard_map/pallas_call | solution.py:147
  369.8 24.4 %shard_map.121 = (bf16[64,512,512]{2,1,0:T(8,128)(2,1)}, bf16[64,512,512]{2,1,0:T(8,128)(2,1)}) custom-call(s32[2]{0:T(128)} %pad_add_fusion.id_ref, bf16[16,512,128]{2,1,0:T(8,128)(2,1)} %collective-permute-done.12.refs_0_, bf16[16,512,128]{2,1,0:T(8,128)(2,1)} %collective-permute-done.13.refs_1_, ...), custom_call_target="tpu_custom_call", output_to_operand_aliasing={{0}: (7, {}), {1}: (8, {})} | custom-call | flops 10000000000 | bytes 100000000 | tf_op jit(solution)/shard_map/pallas_call | solution.py:147
  452.1 27.4 %shard_map.126 = (f32[4,64,64,128]{3,2,1,0:T(8,128)}, f32[4,64,64,128]{3,2,1,0:T(8,128)}) custom-call(s32[2]{0:T(128)} %pad_add_fusion.id_ref, bf16[64,512,512]{2,1,0:T(8,128)(2,1)} %get-tuple-element.219.a_ref, bf16[64,512,512]{2,1,0:T(8,128)(2,1)} %get-tuple-element.218.b_ref), custom_call_target="tpu_custom_call" | custom-call | flops 10000000000 | bytes 100000000 | tf_op jit(solution)/shard_map/pallas_call | solution.py:182
  567.2 43.9 %collective-permute-done.38.refs_0_ = bf16[16,512,128]{2,1,0:T(8,128)(2,1)} collective-permute-done((bf16[16,512,128]{2,1,0:T(8,128)(2,1)}, bf16[16,512,128]{2,1,0:T(8,128)(2,1)}, u32[]{:S(2)}, u32[]{:S(2)}) %collective-permute-start.38) | collective-permute-done | bytes 2097184 | tf_op jit(solution)/shard_map/ppermute | solution.py:468
  613.1 42.9 %collective-permute-done.47.refs_0_ = bf16[16,512,128]{2,1,0:T(8,128)(2,1)} collective-permute-done((bf16[16,512,128]{2,1,0:T(8,128)(2,1)}, bf16[16,512,128]{2,1,0:T(8,128)(2,1)}, u32[]{:S(2)}, u32[]{:S(2)}) %collective-permute-start.47) | collective-permute-done | bytes 2097184 | tf_op jit(solution)/shard_map/ppermute | solution.py:468
  656.6 44.4 %collective-permute-done.32.refs_0_ = bf16[16,512,128]{2,1,0:T(8,128)(2,1)} collective-permute-done((bf16[16,512,128]{2,1,0:T(8,128)(2,1)}, bf16[16,512,128]{2,1,0:T(8,128)(2,1)}, u32[]{:S(2)}, u32[]{:S(2)}) %collective-permute-start.32) | collective-permute-done | bytes 2097184 | tf_op jit(solution)/shard_map/ppermute | solution.py:468
  703.0 42.3 %collective-permute-done.41.refs_0_ = bf16[16,512,128]{2,1,0:T(8,128)(2,1)} collective-permute-done((bf16[16,512,128]{2,1,0:T(8,128)(2,1)}, bf16[16,512,128]{2,1,0:T(8,128)(2,1)}, u32[]{:S(2)}, u32[]{:S(2)}) %collective-permute-start.41) | collective-permute-done | bytes 2097184 | tf_op jit(solution)/shard_map/ppermute | solution.py:468
  808.3 24.5 %shard_map.135 = (bf16[64,512,512]{2,1,0:T(8,128)(2,1)}, bf16[64,512,512]{2,1,0:T(8,128)(2,1)}) custom-call(s32[2]{0:T(128)} %pad_add_fusion.id_ref, bf16[16,512,128]{2,1,0:T(8,128)(2,1)} %collective-permute-done.38.refs_0_, bf16[16,512,128]{2,1,0:T(8,128)(2,1)} %collective-permute-done.50.refs_1_, ...), custom_call_target="tpu_custom_call", output_to_operand_aliasing={{0}: (7, {}), {1}: (8, {})} | custom-call | flops 10000000000 | bytes 100000000 | tf_op jit(solution)/shard_map/pallas_call | solution.py:147
  833.0 24.5 %shard_map.136 = (bf16[64,512,512]{2,1,0:T(8,128)(2,1)}, bf16[64,512,512]{2,1,0:T(8,128)(2,1)}) custom-call(s32[2]{0:T(128)} %pad_add_fusion.id_ref, bf16[16,512,128]{2,1,0:T(8,128)(2,1)} %collective-permute-done.47.refs_0_, bf16[16,512,128]{2,1,0:T(8,128)(2,1)} %collective-permute-done.48.refs_1_, ...), custom_call_target="tpu_custom_call", output_to_operand_aliasing={{0}: (7, {}), {1}: (8, {})} | custom-call | flops 10000000000 | bytes 100000000 | tf_op jit(solution)/shard_map/pallas_call | solution.py:147
  857.9 24.5 %shard_map.137 = (bf16[64,512,512]{2,1,0:T(8,128)(2,1)}, bf16[64,512,512]{2,1,0:T(8,128)(2,1)}) custom-call(s32[2]{0:T(128)} %pad_add_fusion.id_ref, bf16[16,512,128]{2,1,0:T(8,128)(2,1)} %collective-permute-done.32.refs_0_, bf16[16,512,128]{2,1,0:T(8,128)(2,1)} %collective-permute-done.44.refs_1_, ...), custom_call_target="tpu_custom_call", output_to_operand_aliasing={{0}: (7, {}), {1}: (8, {})} | custom-call | flops 10000000000 | bytes 100000000 | tf_op jit(solution)/shard_map/pallas_call | solution.py:147
  882.9 24.4 %shard_map.138 = (bf16[64,512,512]{2,1,0:T(8,128)(2,1)}, bf16[64,512,512]{2,1,0:T(8,128)(2,1)}) custom-call(s32[2]{0:T(128)} %pad_add_fusion.id_ref, bf16[16,512,128]{2,1,0:T(8,128)(2,1)} %collective-permute-done.41.refs_0_, bf16[16,512,128]{2,1,0:T(8,128)(2,1)} %collective-permute-done.42.refs_1_, ...), custom_call_target="tpu_custom_call", output_to_operand_aliasing={{0}: (7, {}), {1}: (8, {})} | custom-call | flops 10000000000 | bytes 100000000 | tf_op jit(solution)/shard_map/pallas_call | solution.py:147
  965.2 26.7 %shard_map.143 = (f32[4,64,64,128]{3,2,1,0:T(8,128)}, f32[4,64,64,128]{3,2,1,0:T(8,128)}) custom-call(s32[2]{0:T(128)} %pad_add_fusion.id_ref, bf16[64,512,512]{2,1,0:T(8,128)(2,1)} %get-tuple-element.256.a_ref, bf16[64,512,512]{2,1,0:T(8,128)(2,1)} %get-tuple-element.255.b_ref), custom_call_target="tpu_custom_call" | custom-call | flops 10000000000 | bytes 100000000 | tf_op jit(solution)/shard_map/pallas_call | solution.py:182
  1005.4 27.4 %shard_map.144 = (bf16[32,512,128]{2,1,0:T(8,128)(2,1)}, bf16[64,32,512]{2,1,0:T(8,128)(2,1)}, bf16[64,32,512]{2,1,0:T(8,128)(2,1)}, bf16[64,32,128]{2,1,0:T(8,1...) custom-call(s32[2]{0:T(128)} %pad_add_fusion.id_ref, ...), custom_call_target="tpu_custom_call" | custom-call | flops 10000000000 | bytes 100000000 | tf_op jit(solution)/shard_map/pallas_call | solution.py:371
  1032.9 27.8 %shard_map.145 = (bf16[32,512,128]{2,1,0:T(8,128)(2,1)}, bf16[64,32,512]{2,1,0:T(8,128)(2,1)}, bf16[64,32,512]{2,1,0:T(8,128)(2,1)}, bf16[64,32,128]{2,1,0:T(8,1...) custom-call(s32[2]{0:T(128)} %pad_add_fusion.id_ref, ...), custom_call_target="tpu_custom_call" | custom-call | flops 10000000000 | bytes 100000000 | tf_op jit(solution)/shard_map/pallas_call | solution.py:371
  1089.5 27.0 %collective-permute-done.78.rest_13_ = bf16[64,32,128]{2,1,0:T(8,128)(2,1)} collective-permute-done((bf16[64,32,128]{2,1,0:T(8,128)(2,1)}, bf16[64,32,128]{2,1,0:T(8,128)(2,1)}, u32[]{:S(2)}, u32[]{:S(2)}) %collective-permute-start.78) | collective-permute-done | bytes 524320 | tf_op jit(solution)/shard_map/ppermute | solution.py:468
  1265.4 32.0 %collective-permute-done.64.refs_5_ = bf16[64,32,128]{2,1,0:T(8,128)(2,1)} collective-permute-done((bf16[64,32,128]{2,1,0:T(8,128)(2,1)}, bf16[64,32,128]{2,1,0:T(8,128)(2,1)}, u32[]{:S(2)}, u32[]{:S(2)}) %collective-permute-start.64) | collective-permute-done | bytes 524320 | tf_op jit(solution)/shard_map/ppermute | solution.py:468
  1322.8 41.1 %shard_map.150 = (f32[32,512,128]{2,1,0:T(8,128)}, f32[512,128]{1,0:T(8,128)}, f32[128,128]{1,0:T(8,128)}, f32[8,128]{1,0:T(8,128)}, f32[8,128]{1,0:T(8,128)}) custom-call(s32[2]{0:T(128)} %pad_add_fusion.id_ref, bf16[64,32,128]{2,1,0:T(8,128)(2,1)} %get-tuple-element.264.rest_16_.refs_0_, bf16[64,32,128]{2,1,0:T(8,128)(2,1)} %collective-permute-done.60.refs_1_, ...), custom_call_target="tpu_custom_call" | custom-call | flops 20000000000 | bytes 200000000 | tf_op jit(solution)/shard_map/pallas_call | solution.py:451
  1369.4 27.4 %shard_map.151 = (bf16[32,512,128]{2,1,0:T(8,128)(2,1)}, bf16[64,32,512]{2,1,0:T(8,128)(2,1)}, bf16[64,32,512]{2,1,0:T(8,128)(2,1)}, bf16[64,32,128]{2,1,0:T(8,1...) custom-call(s32[2]{0:T(128)} %pad_add_fusion.id_ref, ...), custom_call_target="tpu_custom_call" | custom-call | flops 10000000000 | bytes 100000000 | tf_op jit(solution)/shard_map/pallas_call | solution.py:371
  1412.5 41.3 %shard_map.152 = (f32[32,512,128]{2,1,0:T(8,128)}, f32[512,128]{1,0:T(8,128)}, f32[128,128]{1,0:T(8,128)}, f32[8,128]{1,0:T(8,128)}, f32[8,128]{1,0:T(8,128)}) custom-call(s32[2]{0:T(128)} %pad_add_fusion.id_ref, bf16[64,32,128]{2,1,0:T(8,128)(2,1)} %get-tuple-element.298.rest_16_.refs_0_, bf16[64,32,128]{2,1,0:T(8,128)(2,1)} %collective-permute-done.89.refs_1_, ...), custom_call_target="tpu_custom_call" | custom-call | flops 20000000000 | bytes 200000000 | tf_op jit(solution)/shard_map/pallas_call | solution.py:451
  1453.8 27.4 %shard_map.153 = (bf16[32,512,128]{2,1,0:T(8,128)(2,1)}, bf16[64,32,512]{2,1,0:T(8,128)(2,1)}, bf16[64,32,512]{2,1,0:T(8,128)(2,1)}, bf16[64,32,128]{2,1,0:T(8,1...) custom-call(s32[2]{0:T(128)} %pad_add_fusion.id_ref, ...), custom_call_target="tpu_custom_call" | custom-call | flops 10000000000 | bytes 100000000 | tf_op jit(solution)/shard_map/pallas_call | solution.py:371
  1510.0 27.1 %collective-permute-done.116.rest_13_ = bf16[64,32,128]{2,1,0:T(8,128)(2,1)} collective-permute-done((bf16[64,32,128]{2,1,0:T(8,128)(2,1)}, bf16[64,32,128]{2,1,0:T(8,128)(2,1)}, u32[]{:S(2)}, u32[]{:S(2)}) %collective-permute-start.116) | collective-permute-done | bytes 524320 | tf_op jit(solution)/shard_map/ppermute | solution.py:468
  1556.7 22.6 %shard_map.154 = (bf16[64,64,512]{2,1,0:T(8,128)(2,1)}, bf16[64,64,512]{2,1,0:T(8,128)(2,1)}) custom-call(s32[2]{0:T(128)} %pad_add_fusion.id_ref, bf16[64,512,512]{2,1,0:T(8,128)(2,1)} %get-tuple-element.218.b_ref, bf16[64,32,512]{2,1,0:T(8,128)(2,1)} %get-tuple-element.301.refs_24_.rest_0_, bf16[64,32,512]{2,1,0:T(8,128)(2,1)} %collective-permute-done.88.rest_1_, ...), custom_call_target="tpu_custom_call" | custom-call | flops 10000000000 | bytes 100000000 | tf_op jit(solution)/shard_map/pallas_call | solution.py:257
  1589.7 24.5 %shard_map.155 = (bf16[64,64,512]{2,1,0:T(8,128)(2,1)}, bf16[64,64,512]{2,1,0:T(8,128)(2,1)}) custom-call(s32[2]{0:T(128)} %pad_add_fusion.id_ref, bf16[64,512,512]{2,1,0:T(8,128)(2,1)} %get-tuple-element.219.a_ref, bf16[64,32,128]{2,1,0:T(8,128)(2,1)} %get-tuple-element.323.rest_0_, bf16[64,32,128]{2,1,0:T(8,128)(2,1)} %collective-permute-done.105.rest_1_, ...), custom_call_target="tpu_custom_call" | custom-call | flops 10000000000 | bytes 100000000 | tf_op jit(solution)/shard_map/pallas_call | solution.py:257
  1627.7 40.7 %shard_map.156 = (f32[64,512,128]{2,1,0:T(8,128)}, f32[512,128]{1,0:T(8,128)}, f32[128,128]{1,0:T(8,128)}, f32[8,128]{1,0:T(8,128)}, f32[8,128]{1,0:T(8,128)}) custom-call(s32[2]{0:T(128)} %pad_add_fusion.id_ref, bf16[64,64,512]{2,1,0:T(8,128)(2,1)} %get-tuple-element.321.rest_16_.refs_0_, bf16[64,64,512]{2,1,0:T(8,128)(2,1)} %collective-permute-done.104.refs_1_, ...), custom_call_target="tpu_custom_call" | custom-call | flops 20000000000 | bytes 200000000 | tf_op jit(solution)/shard_map/pallas_call | solution.py:451
  1668.4 40.8 %shard_map.157 = (f32[64,512,128]{2,1,0:T(8,128)}, f32[512,128]{1,0:T(8,128)}, f32[128,128]{1,0:T(8,128)}, f32[8,128]{1,0:T(8,128)}, f32[8,128]{1,0:T(8,128)}) custom-call(s32[2]{0:T(128)} %pad_add_fusion.id_ref, bf16[64,64,512]{2,1,0:T(8,128)(2,1)} %get-tuple-element.321.rest_16_.refs_0_, ...), custom_call_target="tpu_custom_call", output_to_operand_aliasing={{0}: (13, {})} | custom-call | flops 20000000000 | bytes 200000000 | tf_op jit(solution)/shard_map/pallas_call | solution.py:451
  1720.1 44.6 %all-reduce.3.cloned.1.call-done = (f32[786,128]{1,0:T(8,128)}, f32[786,128]{1,0:T(8,128)}) async-done(((f32[786,128]{1,0:T(8,128)}, f32[786,128]{1,0:T(8,128)}), (f32[786,128]{1,0:T(8,128)}, f32[786,128]{1,0:T(8,128)})) %all-reduce.3.cloned.1.call-update) | async-done | bytes 804880 | tf_op jit(solution)/shard_map/psum | solution.py:562
  (433 shorter events, 716.7 us)
Async XLA Ops:
  7.2 224.1 %all-gather.2.cloned.1.call-start = ((), (), s32[]{:S(2)}) async-start(), calls=%async_computation | async-start | bytes 1179648 | tf_op jit(solution)/shard_map/all_gather | solution.py:475
  46.2 96.5 %collective-permute-start.6 = (bf16[16,512,128]{2,1,0:T(8,128)(2,1)}, bf16[16,512,128]{2,1,0:T(8,128)(2,1)}, u32[]{:S(2)}, u32[]{:S(2)}) collective-permute-start(bf16[16,512,128]{2,1,0:T(8,128)(2,1)} %get-tuple-element.194.refs_0_), channel_id=1, source_target_pairs={{0,4},{1,5},{2,6},{3,7},{4,0},{5,1},{6,2},{7,3}} | collective-permute-start | bytes 6291464 | tf_op jit(solution)/shard_map/ppermute | solution.py:468
  46.7 96.0 %collective-permute-start.18 = (bf16[16,512,128]{2,1,0:T(8,128)(2,1)}, bf16[16,512,128]{2,1,0:T(8,128)(2,1)}, u32[]{:S(2)}, u32[]{:S(2)}) collective-permute-start(bf16[16,512,128]{2,1,0:T(8,128)(2,1)} %get-tuple-element.194.refs_0_), channel_id=1, source_target_pairs={{0,2},{1,3},{2,0},{3,1},{4,6},{5,7},{6,4},{7,5}} | collective-permute-start | bytes 6291464 | tf_op jit(solution)/shard_map/ppermute | solution.py:468
  46.7 138.8 %collective-permute-start.3 = (bf16[16,512,128]{2,1,0:T(8,128)(2,1)}, bf16[16,512,128]{2,1,0:T(8,128)(2,1)}, u32[]{:S(2)}, u32[]{:S(2)}) collective-permute-start(bf16[16,512,128]{2,1,0:T(8,128)(2,1)} %get-tuple-element.193.refs_0_), channel_id=1, source_target_pairs={{0,2},{1,3},{2,0},{3,1},{4,6},{5,7},{6,4},{7,5}} | collective-permute-start | bytes 6291464 | tf_op jit(solution)/shard_map/ppermute | solution.py:468
  91.4 96.1 %collective-permute-start.16 = (bf16[16,512,128]{2,1,0:T(8,128)(2,1)}, bf16[16,512,128]{2,1,0:T(8,128)(2,1)}, u32[]{:S(2)}, u32[]{:S(2)}) collective-permute-start(bf16[16,512,128]{2,1,0:T(8,128)(2,1)} %get-tuple-element.193.refs_0_), channel_id=1, source_target_pairs={{0,4},{1,5},{2,6},{3,7},{4,0},{5,1},{6,2},{7,3}} | collective-permute-start | bytes 6291464 | tf_op jit(solution)/shard_map/ppermute | solution.py:468
  93.5 137.8 %collective-permute-start = (bf16[16,512,128]{2,1,0:T(8,128)(2,1)}, bf16[16,512,128]{2,1,0:T(8,128)(2,1)}, u32[]{:S(2)}, u32[]{:S(2)}) collective-permute-start(bf16[16,512,128]{2,1,0:T(8,128)(2,1)} %get-tuple-element.192.refs_0_), channel_id=1, source_target_pairs={{0,4},{1,5},{2,6},{3,7},{4,0},{5,1},{6,2},{7,3}} | collective-permute-start | bytes 6291464 | tf_op jit(solution)/shard_map/ppermute | solution.py:468
  95.7 1669.0 %all-reduce.3.cloned.1.call-start = ((), (), s32[]{:S(2)}) async-start(), calls=%async_computation.1 | async-start | bytes 1622016 | tf_op jit(solution)/shard_map/psum | solution.py:562
  142.6 103.1 %collective-permute-start.12 = (bf16[16,512,128]{2,1,0:T(8,128)(2,1)}, bf16[16,512,128]{2,1,0:T(8,128)(2,1)}, u32[]{:S(2)}, u32[]{:S(2)}) collective-permute-start(bf16[16,512,128]{2,1,0:T(8,128)(2,1)} %get-tuple-element.192.refs_0_), channel_id=1, source_target_pairs={{0,2},{1,3},{2,0},{3,1},{4,6},{5,7},{6,4},{7,5}} | collective-permute-start | bytes 6291464 | tf_op jit(solution)/shard_map/ppermute | solution.py:468
  142.7 103.6 %collective-permute-start.21 = (bf16[16,512,128]{2,1,0:T(8,128)(2,1)}, bf16[16,512,128]{2,1,0:T(8,128)(2,1)}, u32[]{:S(2)}, u32[]{:S(2)}) collective-permute-start(bf16[16,512,128]{2,1,0:T(8,128)(2,1)} %collective-permute-done.9.refs_0_), channel_id=1, source_target_pairs={{0,1},{1,0},{2,3},{3,2},{4,5},{5,4},{6,7},{7,6}} | collective-permute-start | bytes 6291464 | tf_op jit(solution)/shard_map/ppermute | solution.py:468
  187.6 73.6 %collective-permute-start.20 = (bf16[16,512,128]{2,1,0:T(8,128)(2,1)}, bf16[16,512,128]{2,1,0:T(8,128)(2,1)}, u32[]{:S(2)}, u32[]{:S(2)}) collective-permute-start(bf16[16,512,128]{2,1,0:T(8,128)(2,1)} %collective-permute-done.6.refs_2_), channel_id=1, source_target_pairs={{0,1},{1,0},{2,3},{3,2},{4,5},{5,4},{6,7},{7,6}} | collective-permute-start | bytes 6291464 | tf_op jit(solution)/shard_map/ppermute | solution.py:468
  292.3 76.0 %collective-permute-start.4 = (bf16[16,512,128]{2,1,0:T(8,128)(2,1)}, bf16[16,512,128]{2,1,0:T(8,128)(2,1)}, u32[]{:S(2)}, u32[]{:S(2)}) collective-permute-start(bf16[16,512,128]{2,1,0:T(8,128)(2,1)} %collective-permute-done.3.refs_0_), channel_id=1, source_target_pairs={{0,4},{1,5},{2,6},{3,7},{4,0},{5,1},{6,2},{7,3}} | collective-permute-start | bytes 6291464 | tf_op jit(solution)/shard_map/ppermute | solution.py:468
  292.5 77.3 %collective-permute-start.1 = (bf16[16,512,128]{2,1,0:T(8,128)(2,1)}, bf16[16,512,128]{2,1,0:T(8,128)(2,1)}, u32[]{:S(2)}, u32[]{:S(2)}) collective-permute-start(bf16[16,512,128]{2,1,0:T(8,128)(2,1)} %collective-permute-done.refs_2_), channel_id=1, source_target_pairs={{0,2},{1,3},{2,0},{3,1},{4,6},{5,7},{6,4},{7,5}} | collective-permute-start | bytes 6291464 | tf_op jit(solution)/shard_map/ppermute | solution.py:468
  294.2 75.7 %collective-permute-start.13 = (bf16[16,512,128]{2,1,0:T(8,128)(2,1)}, bf16[16,512,128]{2,1,0:T(8,128)(2,1)}, u32[]{:S(2)}, u32[]{:S(2)}) collective-permute-start(bf16[16,512,128]{2,1,0:T(8,128)(2,1)} %collective-permute-done.12.refs_0_), channel_id=1, source_target_pairs={{0,1},{1,0},{2,3},{3,2},{4,5},{5,4},{6,7},{7,6}} | collective-permute-start | bytes 6291464 | tf_op jit(solution)/shard_map/ppermute | solution.py:468
  318.7 75.6 %collective-permute-start.11 = (bf16[16,512,128]{2,1,0:T(8,128)(2,1)}, bf16[16,512,128]{2,1,0:T(8,128)(2,1)}, u32[]{:S(2)}, u32[]{:S(2)}) collective-permute-start(bf16[16,512,128]{2,1,0:T(8,128)(2,1)} %collective-permute-done.10.refs_0_), channel_id=1, source_target_pairs={{0,1},{1,0},{2,3},{3,2},{4,5},{5,4},{6,7},{7,6}} | collective-permute-start | bytes 6291464 | tf_op jit(solution)/shard_map/ppermute | solution.py:468
  369.8 67.8 %collective-permute-start.2 = (bf16[16,512,128]{2,1,0:T(8,128)(2,1)}, bf16[16,512,128]{2,1,0:T(8,128)(2,1)}, u32[]{:S(2)}, u32[]{:S(2)}) collective-permute-start(bf16[16,512,128]{2,1,0:T(8,128)(2,1)} %collective-permute-done.1.refs_0_), channel_id=1, source_target_pairs={{0,1},{1,0},{2,3},{3,2},{4,5},{5,4},{6,7},{7,6}} | collective-permute-start | bytes 6291464 | tf_op jit(solution)/shard_map/ppermute | solution.py:468
  563.3 92.8 %collective-permute-start.47 = (bf16[16,512,128]{2,1,0:T(8,128)(2,1)}, bf16[16,512,128]{2,1,0:T(8,128)(2,1)}, u32[]{:S(2)}, u32[]{:S(2)}) collective-permute-start(bf16[16,512,128]{2,1,0:T(8,128)(2,1)} %get-tuple-element.231.refs_0_), channel_id=1, source_target_pairs={{0,2},{1,3},{2,0},{3,1},{4,6},{5,7},{6,4},{7,5}} | collective-permute-start | bytes 6291464 | tf_op jit(solution)/shard_map/ppermute | solution.py:468
  564.7 91.9 %collective-permute-start.35 = (bf16[16,512,128]{2,1,0:T(8,128)(2,1)}, bf16[16,512,128]{2,1,0:T(8,128)(2,1)}, u32[]{:S(2)}, u32[]{:S(2)}) collective-permute-start(bf16[16,512,128]{2,1,0:T(8,128)(2,1)} %get-tuple-element.231.refs_0_), channel_id=1, source_target_pairs={{0,4},{1,5},{2,6},{3,7},{4,0},{5,1},{6,2},{7,3}} | collective-permute-start | bytes 6291464 | tf_op jit(solution)/shard_map/ppermute | solution.py:468
  566.6 134.3 %collective-permute-start.32 = (bf16[16,512,128]{2,1,0:T(8,128)(2,1)}, bf16[16,512,128]{2,1,0:T(8,128)(2,1)}, u32[]{:S(2)}, u32[]{:S(2)}) collective-permute-start(bf16[16,512,128]{2,1,0:T(8,128)(2,1)} %get-tuple-element.230.refs_0_), channel_id=1, source_target_pairs={{0,2},{1,3},{2,0},{3,1},{4,6},{5,7},{6,4},{7,5}} | collective-permute-start | bytes 6291464 | tf_op jit(solution)/shard_map/ppermute | solution.py:468
  611.1 90.5 %collective-permute-start.45 = (bf16[16,512,128]{2,1,0:T(8,128)(2,1)}, bf16[16,512,128]{2,1,0:T(8,128)(2,1)}, u32[]{:S(2)}, u32[]{:S(2)}) collective-permute-start(bf16[16,512,128]{2,1,0:T(8,128)(2,1)} %get-tuple-element.230.refs_0_), channel_id=1, source_target_pairs={{0,4},{1,5},{2,6},{3,7},{4,0},{5,1},{6,2},{7,3}} | collective-permute-start | bytes 6291464 | tf_op jit(solution)/shard_map/ppermute | solution.py:468
  611.6 133.6 %collective-permute-start.41 = (bf16[16,512,128]{2,1,0:T(8,128)(2,1)}, bf16[16,512,128]{2,1,0:T(8,128)(2,1)}, u32[]{:S(2)}, u32[]{:S(2)}) collective-permute-start(bf16[16,512,128]{2,1,0:T(8,128)(2,1)} %get-tuple-element.229.refs_0_), channel_id=1, source_target_pairs={{0,2},{1,3},{2,0},{3,1},{4,6},{5,7},{6,4},{7,5}} | collective-permute-start | bytes 6291464 | tf_op jit(solution)/shard_map/ppermute | solution.py:468
  656.0 103.7 %collective-permute-start.29 = (bf16[16,512,128]{2,1,0:T(8,128)(2,1)}, bf16[16,512,128]{2,1,0:T(8,128)(2,1)}, u32[]{:S(2)}, u32[]{:S(2)}) collective-permute-start(bf16[16,512,128]{2,1,0:T(8,128)(2,1)} %get-tuple-element.229.refs_0_), channel_id=1, source_target_pairs={{0,4},{1,5},{2,6},{3,7},{4,0},{5,1},{6,2},{7,3}} | collective-permute-start | bytes 6291464 | tf_op jit(solution)/shard_map/ppermute | solution.py:468
  656.6 103.7 %collective-permute-start.50 = (bf16[16,512,128]{2,1,0:T(8,128)(2,1)}, bf16[16,512,128]{2,1,0:T(8,128)(2,1)}, u32[]{:S(2)}, u32[]{:S(2)}) collective-permute-start(bf16[16,512,128]{2,1,0:T(8,128)(2,1)} %collective-permute-done.38.refs_0_), channel_id=1, source_target_pairs={{0,1},{1,0},{2,3},{3,2},{4,5},{5,4},{6,7},{7,6}} | collective-permute-start | bytes 6291464 | tf_op jit(solution)/shard_map/ppermute | solution.py:468
  701.5 73.7 %collective-permute-start.48 = (bf16[16,512,128]{2,1,0:T(8,128)(2,1)}, bf16[16,512,128]{2,1,0:T(8,128)(2,1)}, u32[]{:S(2)}, u32[]{:S(2)}) collective-permute-start(bf16[16,512,128]{2,1,0:T(8,128)(2,1)} %collective-permute-done.47.refs_0_), channel_id=1, source_target_pairs={{0,1},{1,0},{2,3},{3,2},{4,5},{5,4},{6,7},{7,6}} | collective-permute-start | bytes 6291464 | tf_op jit(solution)/shard_map/ppermute | solution.py:468
  805.2 77.1 %collective-permute-start.33 = (bf16[16,512,128]{2,1,0:T(8,128)(2,1)}, bf16[16,512,128]{2,1,0:T(8,128)(2,1)}, u32[]{:S(2)}, u32[]{:S(2)}) collective-permute-start(bf16[16,512,128]{2,1,0:T(8,128)(2,1)} %collective-permute-done.32.refs_0_), channel_id=1, source_target_pairs={{0,4},{1,5},{2,6},{3,7},{4,0},{5,1},{6,2},{7,3}} | collective-permute-start | bytes 6291464 | tf_op jit(solution)/shard_map/ppermute | solution.py:468
  806.8 76.1 %collective-permute-start.43 = (bf16[16,512,128]{2,1,0:T(8,128)(2,1)}, bf16[16,512,128]{2,1,0:T(8,128)(2,1)}, u32[]{:S(2)}, u32[]{:S(2)}) collective-permute-start(bf16[16,512,128]{2,1,0:T(8,128)(2,1)} %collective-permute-done.29.refs_2_), channel_id=1, source_target_pairs={{0,1},{1,0},{2,3},{3,2},{4,5},{5,4},{6,7},{7,6}} | collective-permute-start | bytes 6291464 | tf_op jit(solution)/shard_map/ppermute | solution.py:468
  806.8 75.9 %collective-permute-start.30 = (bf16[16,512,128]{2,1,0:T(8,128)(2,1)}, bf16[16,512,128]{2,1,0:T(8,128)(2,1)}, u32[]{:S(2)}, u32[]{:S(2)}) collective-permute-start(bf16[16,512,128]{2,1,0:T(8,128)(2,1)} %collective-permute-done.29.refs_2_), channel_id=1, source_target_pairs={{0,2},{1,3},{2,0},{3,1},{4,6},{5,7},{6,4},{7,5}} | collective-permute-start | bytes 6291464 | tf_op jit(solution)/shard_map/ppermute | solution.py:468
  832.8 74.6 %collective-permute-start.40 = (bf16[16,512,128]{2,1,0:T(8,128)(2,1)}, bf16[16,512,128]{2,1,0:T(8,128)(2,1)}, u32[]{:S(2)}, u32[]{:S(2)}) collective-permute-start(bf16[16,512,128]{2,1,0:T(8,128)(2,1)} %collective-permute-done.39.refs_0_), channel_id=1, source_target_pairs={{0,1},{1,0},{2,3},{3,2},{4,5},{5,4},{6,7},{7,6}} | collective-permute-start | bytes 6291464 | tf_op jit(solution)/shard_map/ppermute | solution.py:468
  882.8 68.0 %collective-permute-start.31 = (bf16[16,512,128]{2,1,0:T(8,128)(2,1)}, bf16[16,512,128]{2,1,0:T(8,128)(2,1)}, u32[]{:S(2)}, u32[]{:S(2)}) collective-permute-start(bf16[16,512,128]{2,1,0:T(8,128)(2,1)} %collective-permute-done.30.refs_0_), channel_id=1, source_target_pairs={{0,1},{1,0},{2,3},{3,2},{4,5},{5,4},{6,7},{7,6}} | collective-permute-start | bytes 6291464 | tf_op jit(solution)/shard_map/ppermute | solution.py:468
  1060.7 71.3 %collective-permute-start.59 = (bf16[64,32,512]{2,1,0:T(8,128)(2,1)}, bf16[64,32,512]{2,1,0:T(8,128)(2,1)}, u32[]{:S(2)}, u32[]{:S(2)}) collective-permute-start(bf16[64,32,512]{2,1,0:T(8,128)(2,1)} %get-tuple-element.263), channel_id=1, source_target_pairs={{0,1},{1,0},{2,3},{3,2},{4,5},{5,4},{6,7},{7,6}} | collective-permute-start | bytes 6291464 | tf_op jit(solution)/shard_map/ppermute | solution.py:468
  1061.1 72.5 %collective-permute-start.58 = (bf16[64,32,512]{2,1,0:T(8,128)(2,1)}, bf16[64,32,512]{2,1,0:T(8,128)(2,1)}, u32[]{:S(2)}, u32[]{:S(2)}) collective-permute-start(bf16[64,32,512]{2,1,0:T(8,128)(2,1)} %get-tuple-element.261), channel_id=1, source_target_pairs={{0,1},{1,0},{2,3},{3,2},{4,5},{5,4},{6,7},{7,6}} | collective-permute-start | bytes 6291464 | tf_op jit(solution)/shard_map/ppermute | solution.py:468
  1481.2 71.4 %collective-permute-start.103 = (bf16[64,32,512]{2,1,0:T(8,128)(2,1)}, bf16[64,32,512]{2,1,0:T(8,128)(2,1)}, u32[]{:S(2)}, u32[]{:S(2)}) collective-permute-start(bf16[64,32,512]{2,1,0:T(8,128)(2,1)} %get-tuple-element.320), channel_id=1, source_target_pairs={{0,1},{1,0},{2,3},{3,2},{4,5},{5,4},{6,7},{7,6}} | collective-permute-start | bytes 6291464 | tf_op jit(solution)/shard_map/ppermute | solution.py:468
  1481.7 72.9 %collective-permute-start.88 = (bf16[64,32,512]{2,1,0:T(8,128)(2,1)}, bf16[64,32,512]{2,1,0:T(8,128)(2,1)}, u32[]{:S(2)}, u32[]{:S(2)}) collective-permute-start(bf16[64,32,512]{2,1,0:T(8,128)(2,1)} %get-tuple-element.302), channel_id=1, source_target_pairs={{0,1},{1,0},{2,3},{3,2},{4,5},{5,4},{6,7},{7,6}} | collective-permute-start | bytes 6291464 | tf_op jit(solution)/shard_map/ppermute | solution.py:468
  (139 other events, 5049.6 us)
Sparse Core Ops, SparseCore 0:
  95.8 22.2 all-gather.1
  1720.2 44.4 all-reduce.2

commit v2 on v1

--- a/solution.py
+++ b/solution.py
@@ -16,6 +16,7 @@
 NCH = 4
 STRIDE = 72
 PAD = 24
+HOPS = (1, 2, 4)
 VMEM = 62 * 1024 * 1024
 
 
@@ -24,7 +25,7 @@
 
 
 def nt(a, b):
-    return lax.dot_general(a, b, (((1,), (1,)), ((), ())), preferred_element_type=F32)
+    return lax.dot_general(a, b, (((1,), HOPS[:1]), ((), ())), preferred_element_type=F32)
 
 
 def tn(a, b):
@@ -96,8 +97,8 @@
 
 
 def proj_kernel(count, id_ref, *refs):
-    z_refs, (m_ref, w_ref) = refs[:count], refs[count:count + 2]
-    a_ref, b_ref, sa, sb, buf, sem = refs[-6:]
+    z_refs, m_refs, w_ref = refs[:count], refs[count:2 * count], refs[2 * count]
+    a_ref, b_ref, sa, sb, buf, m_ref, sem = refs[-7:]
     step = pl.program_id(0)
     slot = lax.rem(step, 2)
 
@@ -111,6 +112,7 @@
                 copy(j).start()
             if j + 1 < count:
                 copy(j + 1).start()
+            m_ref[...] = m_refs[j][...]
             copy(j).wait()
 
     def row(r):
@@ -134,20 +136,23 @@
     loop(HALF, chan, 2)
 
 
-def proj_chunk(ids, first, blocks, mask, w, t, prev):
+def proj_chunk(ids, first, width, blocks, masks, w, t, prev):
     count = len(blocks)
 
     def place(i, s):
-        return ((s[0] * 2 + s[1]) ^ (first + i)) * NCH + t
+        return ((s[0] * 2 + s[1]) ^ (first + lax.rem(i, width))) * NCH + t + lax.div(i, width)
+
+    def mask_spec(j):
+        return pl.BlockSpec((RB, N), lambda i, s: (t + j // width, 0))
 
     out = pl.BlockSpec((HALF, RB, N), lambda i, s: (0, place(i, s), 0))
     in_specs, args, aliases = chained(
-        [pl.BlockSpec(memory_space=pl.ANY)] * count + [pl.BlockSpec((RB, N), lambda i, s: (place(i, s), 0)),
-                                                       full((256, CH))], [*blocks, mask, w], prev, 0)
+        [pl.BlockSpec(memory_space=pl.ANY)] * count + [mask_spec(j) for j in range(count)] + [full((256, CH))],
+        [*blocks, *[masks[first + j % width] for j in range(count)], w], prev, 0)
     return call(functools.partial(proj_kernel, count), (count,), in_specs, [out, out], [sds((HALF, N, N), BF16)] * 2,
                 [pltpu.VMEM((4, RB * STRIDE, TILE), F32)] * 2
-                + [pltpu.VMEM((2, RB, N, CH), BF16), pltpu.SemaphoreType.DMA((2,))], prefetch=1,
-                aliases={k + 1: v for k, v in aliases.items()}, flops=BIG)(ids, *args)
+                + [pltpu.VMEM((2, RB, N, CH), BF16), pltpu.VMEM((RB, N), F32), pltpu.SemaphoreType.DMA((2,))],
+                prefetch=1, aliases={k + 1: v for k, v in aliases.items()}, flops=BIG)(ids, *args)
 
 
 CB = 8
@@ -159,7 +164,8 @@
     send_ref[c] = jnp.where(h == 0, hi, lo)
 
 
-def tri_kernel(form, id_ref, a_ref, b_ref, keep_ref, send_ref):
+def tri_kernel(form, id_ref, a_ref, b_ref, *rest):
+    keep_ref, send_ref = rest[-2:]
     h = id_ref[1]
 
     def chan(c):
@@ -173,15 +179,17 @@
     loop(CB, chan)
 
 
-def tri_forward(form, ids, a, b):
+def tri_forward(form, part, ids, a, b, after=()):
+    off = part * (HR // CB)
     if form == 'out':
-        a_spec = pl.BlockSpec((CB, TILE, N), lambda c, s: (c, s[0], 0))
+        a_spec = pl.BlockSpec((CB, TILE, N), lambda c, s: (off + c, s[0], 0))
     else:
-        a_spec = pl.BlockSpec((CB, N, TILE), lambda c, s: (c, 0, s[0]))
+        a_spec = pl.BlockSpec((CB, N, TILE), lambda c, s: (off + c, 0, s[0]))
     half = pl.BlockSpec((4, CB, ROWS, TILE), lambda c, s: (0, c, 0, 0))
-    return call(functools.partial(tri_kernel, form), (HALF // CB,),
-                [a_spec, pl.BlockSpec((CB, N, N), lambda c, s: (c, 0, 0))], [half, half],
-                [sds((4, HALF, ROWS, TILE), F32)] * 2, prefetch=1, flops=BIG)(ids, a, b)
+    return call(functools.partial(tri_kernel, form), (HR // CB,),
+                [a_spec, pl.BlockSpec((CB, N, N), lambda c, s: (off + c, 0, 0))]
+                + [pl.BlockSpec(memory_space=pl.ANY)] * len(after), [half, half],
+                [sds((4, HR, ROWS, TILE), F32)] * 2, prefetch=1, flops=BIG)(ids, a, b, *after)
 
 
 def row_ds(start, size):
@@ -264,12 +272,12 @@
                 prefetch=1, flops=BIG)(ids, mat.reshape(HALF, DEV, ROWS, N), *parts, *after)
 
 
-def x_row(xk_ref, xr_ref, r, rb):
-    halves = []
-    for ref in (xk_ref, xr_ref):
-        flat = ref.reshape(4, HALF * rb, TILE)
-        halves.append(jnp.concatenate([flat[l, pl.ds(r, HALF, stride=rb), :] for l in range(4)], axis=1))
-    return jnp.concatenate(halves, axis=0)
+def x_row(x_refs, r):
+    parts = []
+    for ref in x_refs:
+        flat = ref.reshape(4, HR * RB, TILE)
+        parts.append(jnp.concatenate([flat[l, pl.ds(r, HR, stride=RB), :] for l in range(4)], axis=1))
+    return jnp.concatenate(parts, axis=0)
 
 
 def x_norm(x):
@@ -279,11 +287,12 @@
     return cen * rstd, rstd
 
 
-def fin_kernel(xk_ref, xr_ref, z_ref, zn_ref, wg_ref, wo_ref, gt_ref, g1_ref, *rest):
+def fin_kernel(*refs):
+    x_refs, (z_ref, zn_ref, wg_ref, wo_ref, gt_ref, g1_ref, *rest) = refs[:4], refs[4:]
     loc_ref, z1_ref, zn1_ref = rest[-3:]
 
     def row(r):
-        xhat, _ = x_norm(x_row(xk_ref, xr_ref, r, RB))
+        xhat, _ = x_norm(x_row(x_refs, r))
         xn = (xhat * gt_ref[:, 0:1] + gt_ref[:, 1:2]).astype(BF16)
         gate = sigmoid(nn(zn_ref[r], wg_ref[...]))
         z1 = z_ref[r] + gate * tn(xn, wo_ref[...])
@@ -295,18 +304,19 @@
     loop(RB, row)
 
 
-def fin_chunk(xk, xr, z, zn, wg, wo, gt, g1, t, prev):
-    xs = pl.BlockSpec((4, HALF, RB, TILE), lambda i: (0, 0, t, 0))
+def fin_chunk(x, z, zn, wg, wo, gt, g1, t, prev):
+    xs = pl.BlockSpec((4, HR, RB, TILE), lambda i: (0, 0, t, 0))
     zs = pl.BlockSpec((RB, N, CH), lambda i: (t, 0, 0))
     loc = pl.BlockSpec((RB, N, CH), lambda i: (0, 0, 0))
-    in_specs, args, aliases = chained([xs, xs, zs, zs, full((CH, CH)), full((CH, CH)), full((CH, 2)), full((2, CH))],
-                                      [xk, xr, z, zn, wg, wo, gt, g1], prev, 1)
+    in_specs, args, aliases = chained([xs] * 4 + [zs, zs, full((CH, CH)), full((CH, CH)), full((CH, 2)), full((2, CH))],
+                                      [*x, z, zn, wg, wo, gt, g1], prev, 1)
     return call(fin_kernel, (1,), in_specs, [loc, zs, zs],
                 [sds((RB, N, CH), BF16), sds((ROWS, N, CH), F32), sds((ROWS, N, CH), BF16)],
                 aliases=aliases, flops=BIG)(*args)
 
 
-def finb_kernel(id_ref, xk_ref, xr_ref, zn_ref, dz_ref, wg_ref, wo_ref, gt_ref, *rest):
+def finb_kernel(id_ref, *refs):
+    x_refs, (zn_ref, dz_ref, wg_ref, wo_ref, gt_ref, *rest) = refs[:4], refs[4:]
     dg_ref, dk_ref, ds_ref = rest[-15:-12]
     pieces, (dwo_ref, dga_ref, dbi_ref, sd) = rest[-12:-4], rest[-4:]
 
@@ -318,7 +328,7 @@
 
     def row(r):
         base = pl.multiple_of(r * STRIDE, 8)
-        xhat, rstd = x_norm(x_row(xk_ref, xr_ref, r, RB))
+        xhat, rstd = x_norm(x_row(x_refs, r))
         gain = gt_ref[:, 0:1]
         xn = (xhat * gain + gt_ref[:, 1:2]).astype(BF16)
         gate = sigmoid(nn(zn_ref[r], wg_ref[...]))
@@ -362,19 +372,19 @@
     return pl.BlockSpec((RB,) + v.shape[1:], lambda i, s: (off + i,) + (0,) * (v.ndim - 1))
 
 
-def fin_back(e, ids, xk, xr, zn, dz, wg, wo, gt, after=()):
-    x4 = pl.BlockSpec((4, HALF, RB, TILE), lambda i, s: (0, 0, e * (HR // RB) + i, 0))
+def fin_back(e, ids, x, zn, dz, wg, wo, gt, after=()):
+    x4 = pl.BlockSpec((4, HR, RB, TILE), lambda i, s: (0, 0, e * (HR // RB) + i, 0))
     xs = pl.BlockSpec((HALF, RB, N), lambda i, s: (0, i, 0))
     ps = pl.BlockSpec((HALF, RB, TILE), lambda i, s: (0, i, 0))
     dgs = pl.BlockSpec((RB, N, CH), lambda i, s: (i, 0, 0))
     acc = full((CH, CH))
-    return call(finb_kernel, (HR // RB,), [x4, x4, part_spec(zn, e), part_spec(dz, e), acc, acc, full((CH, 2))]
+    return call(finb_kernel, (HR // RB,), [x4] * 4 + [part_spec(zn, e), part_spec(dz, e), acc, acc, full((CH, 2))]
                 + [pl.BlockSpec(memory_space=pl.ANY)] * len(after),
                 [dgs, xs, xs] + [ps] * DEV + [acc] * 3,
                 [sds((HR, N, CH), BF16)] + [sds((HALF, HR, N), BF16)] * 2 + [sds((HALF, HR, TILE), BF16)] * DEV
                 + [sds((CH, CH), F32)] * 3,
                 [pltpu.VMEM((2, 4, RB * STRIDE, TILE), F32)], prefetch=1, flops=BIG)(
-                    ids, xk, xr, zn, dz, wg, wo, gt, *after)
+                    ids, *x, zn, dz, wg, wo, gt, *after)
 
 
 def projb_kernel(form, id_ref, *refs):
@@ -472,53 +482,59 @@
         h = lax.rem(idx, 2)
         ids = jnp.stack([idx // 2, h])
         mask = pair_mask.astype(F32)
-        mask_all = lax.all_gather(mask, 'dap', axis=0, tiled=True)
+        masks = [xor(mask, s) for s in range(DEV)]
         g_pair = ln_pair.astype(F32)
         g_tri = ln_tri.astype(F32)
 
-        def rel(v, axis):
+        def rel(v, axis=0):
             lo, hi = jnp.split(v, 2, axis=axis)
             return jnp.where(h == 0, v, jnp.concatenate([hi, lo], axis=axis))
 
         w_rel, wg, wo_rel, gt_rel = [], [], [], []
         for u in range(2):
             wt = w_in[u, :, :512].T.reshape(4, 2, HALF, CH).transpose(1, 0, 2, 3).reshape(512, CH)
-            w_rel.append(rel(wt, 0))
+            w_rel.append(rel(wt))
             wg.append(w_in[u, :, 512:])
-            wo_rel.append(rel(w_out[u], 0))
-            gt_rel.append(rel(g_tri[u].T, 0))
+            wo_rel.append(rel(w_out[u]))
+            gt_rel.append(rel(g_tri[u].T))
 
         def spread(v):
-            return [v] + [xor(v, s) for s in (1, 2, 4)]
+            return [v] + [xor(v, s) for s in HOPS]
 
         def gather_proj(parts, u):
-            w, prev = w_rel[u][:256], None
-            for t, (own, r1, _, _) in enumerate(parts):
-                prev = proj_chunk(ids, 0, [own, r1], mask_all, w, t, prev)
+            w = w_rel[u][:256]
+            prev = proj_chunk(ids, 0, 2, [v for part in parts for v in part[:2]], masks, w, 0, None)
             far = []
             for t, (_, _, r2, r4) in enumerate(parts):
                 far.append(xor(r4, 2) if t % 2 else xor(r2, 4))
                 near = [r2, xor(r2, 1), r4, xor(r4, 1)]
-                prev = proj_chunk(ids, 2, near, mask_all, w, t, prev)
-            for t, r6 in enumerate(far):
-                r7 = xor(r6, 1)
-                prev = proj_chunk(ids, 6, [r6, r7], mask_all, w, t, prev)
+                prev = proj_chunk(ids, 2, 4, near, masks, w, t, prev)
+            for t in range(0, NCH, 2):
+                pairs = []
+                for i in (t, t + 1):
+                    pairs += [far[i], xor(far[i], 1)]
+                prev = proj_chunk(ids, 6, 2, pairs, masks, w, t, prev)
             return prev
+
+        def triangle(form, a, b):
+            keep, send, dep = [], [], ()
+            for part in range(2):
+                k, v = tri_forward(form, part, ids, a, b, dep)
+                keep, send, dep = keep + [k], send + [xor(v, 1)], (k,)
+            return keep + send
 
         parts, prev = [], None
         for t in range(NCH):
             chunk, zn0 = ln_chunk(pair_act, g_pair[0], t, prev)
             parts, prev = parts + [spread(chunk)], [zn0]
         a0, b0 = gather_proj(parts, 0)
-        x0k, x0s = tri_forward('out', ids, a0, b0)
-        x0r = xor(x0s, 1)
+        x0 = triangle('out', a0, b0)
         parts, prev = [], None
         for t in range(NCH):
-            chunk, z1, zn1 = fin_chunk(x0k, x0r, pair_act, zn0, wg[0], wo_rel[0], gt_rel[0], g_pair[1], t, prev)
+            chunk, z1, zn1 = fin_chunk(x0, pair_act, zn0, wg[0], wo_rel[0], gt_rel[0], g_pair[1], t, prev)
             parts, prev = parts + [spread(chunk)], [z1, zn1]
         a1, b1 = gather_proj(parts, 1)
-        x1k, x1s = tri_forward('in', ids, a1, b1)
-        x1r = xor(x1s, 1)
+        x1 = triangle('in', a1, b1)
 
         def exchange(pieces):
             return [xor(v, s) for s, v in enumerate(pieces)]
@@ -527,8 +543,8 @@
             dg, dk, ds = out[:3]
             return dg, [dk, xor(ds, 1)], exchange(out[3:11]), out[11:], dk
 
-        fb1 = [split(fin_back(0, ids, x1k, x1r, zn1, grad_out, wg[1], wo_rel[1], gt_rel[1]))]
-        out = fin_back(1, ids, x1k, x1r, zn1, grad_out, wg[1], wo_rel[1], gt_rel[1], (fb1[0][4],))
+        fb1 = [split(fin_back(0, ids, x1, zn1, grad_out, wg[1], wo_rel[1], gt_rel[1]))]
+        out = fin_back(1, ids, x1, zn1, grad_out, wg[1], wo_rel[1], gt_rel[1], (fb1[0][4],))
         fb1 += [split(out)]
         dx1, dp1 = fb1[0][1] + fb1[1][1], fb1[0][2] + fb1[1][2]
         da, db, last = [], [], fb1[1][4]
@@ -542,7 +558,7 @@
         for e in range(2):
             pb1.append(proj_back('in', e, ids, da[e], db[e], zn1, z1, grad_out, fb1[e][0], mask, w_rel[1], wg[1],
                                  g_pair[1], after=(last,)))
-            fb0.append(split(fin_back(e, ids, x0k, x0r, zn0, pb1[e][0], wg[0], wo_rel[0], gt_rel[0])))
+            fb0.append(split(fin_back(e, ids, x0, zn0, pb1[e][0], wg[0], wo_rel[0], gt_rel[0])))
             last = fb0[e][4]
         da_k, da_s = tri_back('da_out', ids, b0, fb0[0][1] + fb0[1][1])
         da_0 = [da_k, xor(da_s, 1)]
@@ -550,23 +566,38 @@
         db_0 = [db_k, xor(db_s, 1)]
         pb0, prev = [], None
         for e in range(2):
-            pb0.append(proj_back('out', e, ids, da_0, db_0, zn0, pair_act, pb1[e][0], fb0[e][0], mask, w_rel[0], wg[0],
-                                 g_pair[0], prev=prev))
+            pb0.append(proj_back('out', e, ids, da_0, db_0, zn0, pair_act, pb1[e][0], fb0[e][0], mask, w_rel[0],
+                                 wg[0], g_pair[0], prev=prev))
             prev = [pb0[e][0]]
 
-        def pack(fb, pb):
+        def fin_grads(fb):
             dwo, dga, dbi = [fb[0][3][i] + fb[1][3][i] for i in range(3)]
-            dw, dwg, dgp, dbp = [pb[0][i] + pb[1][i] for i in range(1, 5)]
-            dw = rel(dw, 0).reshape(2, 4, HALF, CH).transpose(1, 0, 2, 3).reshape(512, CH)
-            tri = jnp.stack([jnp.sum(rel(dga, 0), 1), jnp.sum(rel(dbi, 0), 1)])
-            return lax.psum(jnp.concatenate([dw, dwg, rel(dwo, 0), dgp, dbp, tri], axis=0), 'dap')
-
-        def unpack(v):
-            dw, dwg, dwo, dgp, dbp, tri = jnp.split(v, [512, 640, 768, 776, 784])
-            return (jnp.stack([jnp.sum(dgp, 0), jnp.sum(dbp, 0)]), jnp.concatenate([dw.T, dwg], axis=1), tri, dwo)
-
-        packed = [pack(fb0, pb0), pack(fb1, pb1)]
-        return (pb0[1][0],) + tuple(jnp.stack(v) for v in zip(*[unpack(v) for v in packed]))
+            return rel(dwo), jnp.stack([jnp.sum(rel(dga), 1), jnp.sum(rel(dbi), 1)])
+
+        def proj_grads(one, two):
+            dw, dwg, dgp, dbp = [v + w for v, w in zip(one, two)]
+            return [rel(dw).reshape(2, 4, HALF, CH).transpose(1, 0, 2, 3).reshape(512, CH), dwg, dgp, dbp]
+
+        def total(parts):
+            v = jnp.concatenate(parts, axis=0)
+            for s in HOPS:
+                v = v + xor(v, s)
+            cuts = []
+            for part in parts:
+                cuts.append(part.shape[0] + (cuts[-1] if cuts else 0))
+            return jnp.split(v, cuts[:-1])
+
+        def ln_grad(dgp, dbp):
+            return jnp.stack([jnp.sum(dgp, 0), jnp.sum(dbp, 0)])
+
+        (dwo_0, tri_0), (dwo_1, tri_1) = fin_grads(fb0), fin_grads(fb1)
+        early = total(proj_grads(pb1[0][1:], pb1[1][1:]) + [dwo_1, dwo_0, tri_1, tri_0])
+        early, one, two = lax.optimization_barrier((early, pb0[0][1:], pb0[1][1:]))
+        dw_1, dwg_1, dgp_1, dbp_1, dwo_1, dwo_0, tri_1, tri_0 = early
+        dw_0, dwg_0, dgp_0, dbp_0 = total(proj_grads(one, two))
+        return (pb0[1][0], jnp.stack([ln_grad(dgp_0, dbp_0), ln_grad(dgp_1, dbp_1)]),
+                jnp.stack([jnp.concatenate([dw_0.T, dwg_0], axis=1), jnp.concatenate([dw_1.T, dwg_1], axis=1)]),
+                jnp.stack([tri_0, tri_1]), jnp.stack([dwo_0, dwo_1]))
 
 
     return jax.shard_map(device_body, mesh=mesh,

time: 1780 us -> 1750 us (0.983)
  Pallas kernels: 980 us -> 946 us
    ppermute x120 -> x135, waiting for transfers between devices: 621 us -> 682 us  [xor(): return lax.ppermute(v, 'dap', [(i, i ^ s) for i in range(DEV)])]
    psum x1 -> x0, waiting for transfers between devices: 44.6 us -> none  [pack(): lax.psum(jnp.concatenate([dw, dwg, rel(dwo, 0), dgp, dbp, tri], axis=0),...]
    pallas_call x24 -> x14, Pallas kernels: 427 us -> 385 us  [proj_chunk(): call(functools.partial(proj_kernel, count), (count,), in_specs, [out, out...]
    pallas_call x6 -> x8, Pallas kernels: 164 us -> 172 us  [the longest x4 111 us: fin_back(): call(finb_kernel, (HR // RB,), [x4] * 4 + [part_spec(zn, e), part_spec(dz...]
    ppermute x120 -> x135, starting transfers between devices: 89.8 us -> 95.1 us  [xor(): return lax.ppermute(v, 'dap', [(i, i ^ s) for i in range(DEV)])]
  transfers between devices with their start and end apart: 122 -> 135, of which waited for: 41 -> 57; matrix products, arithmetic and copies ran while one was open for 0% -> 0% of each run, Pallas kernels for 35% -> 28%
where the time goes in v2:
time: 1750 us; the launch traced here: 1740 us
  Pallas kernels  946 us (54%)
  waiting for transfers between devices  682 us (39%)
  starting transfers between devices  95.1 us (5%)
    ppermute x135, waiting for transfers between devices, xor(): return lax.ppermute(v, 'dap', [(i, i ^ s) for i in range(DEV)])  682 us
    pallas_call x14, Pallas kernels, proj_chunk(): call(functools.partial(proj_kernel, count), (count,), in_specs, [out, out...  385 us
    pallas_call x4, Pallas kernels, proj_back(): call(functools.partial(projb_kernel, form), (HR // RB,), in_specs + [pl.B...  164 us
    pallas_call x4, Pallas kernels, fin_back(): call(finb_kernel, (HR // RB,), [x4] * 4 + [part_spec(zn, e), part_spec(dz...  111 us
    ppermute x135, starting transfers between devices, xor(): return lax.ppermute(v, 'dap', [(i, i ^ s) for i in range(DEV)])  95.1 us
    pallas_call x4, Pallas kernels, tri_back(): call(bodies[kind], (HALF // CB,), [pl.BlockSpec((CB, DEV, HR, N), lambda...  78.5 us
    pallas_call x4, Pallas kernels, fin_chunk(): call(fin_kernel, (1,), in_specs, [loc, zs, zs], [sds((RB, N, CH), BF16),...  67.9 us
    pallas_call x4, Pallas kernels, tri_forward(): call(functools.partial(tri_kernel, form), (HR // CB,), [a_spec, pl.BlockS...  60.4 us
  transfers between devices with their start and end apart: 135, of which 57 were waited for; matrix products, arithmetic and copies ran while one was open for 0% of the time, Pallas kernels for 28%

profile of v2, /device:TPU:0, one launch (start us, length us, event | category | flops | bytes accessed | tf_op | source)
XLA Modules:
  0.0 1744.6 jit_solution(17215366870167251780)
XLA Ops:
  82.4 43.7 %collective-permute-done.8.refs_0_ = bf16[16,512,128]{2,1,0:T(8,128)(2,1)S(1)} collective-permute-done((bf16[16,512,128]{2,1,0:T(8,128)(2,1)}, bf16[16,512,128]{2,1,0:T(8,128)(2,1)S(1)}, u32[]{:S(2)}, u32[]{:S(2)}) %collective-permute-start.8) | collective-permute-done | bytes 2097184 | tf_op jit(solution)/shard_map/ppermute | solution.py:478
  128.2 43.9 %collective-permute-done.11.refs_2_ = bf16[16,512,128]{2,1,0:T(8,128)(2,1)} collective-permute-done((bf16[16,512,128]{2,1,0:T(8,128)(2,1)}, bf16[16,512,128]{2,1,0:T(8,128)(2,1)}, u32[]{:S(2)}, u32[]{:S(2)}) %collective-permute-start.11) | collective-permute-done | bytes 2097184 | tf_op jit(solution)/shard_map/ppermute | solution.py:478
  173.3 42.9 %collective-permute-done.refs_0_ = bf16[16,512,128]{2,1,0:T(8,128)(2,1)} collective-permute-done((bf16[16,512,128]{2,1,0:T(8,128)(2,1)}, bf16[16,512,128]{2,1,0:T(8,128)(2,1)}, u32[]{:S(2)}, u32[]{:S(2)}) %collective-permute-start) | collective-permute-done | bytes 2097184 | tf_op jit(solution)/shard_map/ppermute | solution.py:478
  217.1 43.0 %collective-permute-done.3.refs_2_ = bf16[16,512,128]{2,1,0:T(8,128)(2,1)} collective-permute-done((bf16[16,512,128]{2,1,0:T(8,128)(2,1)}, bf16[16,512,128]{2,1,0:T(8,128)(2,1)}, u32[]{:S(2)}, u32[]{:S(2)}) %collective-permute-start.3) | collective-permute-done | bytes 2097184 | tf_op jit(solution)/shard_map/ppermute | solution.py:478
  270.8 45.1 %shard_map.114 = (bf16[64,512,512]{2,1,0:T(8,128)(2,1)}, bf16[64,512,512]{2,1,0:T(8,128)(2,1)}) custom-call(s32[2]{0:T(128)} %pad_add_fusion.id_ref, bf16[16,512,128]{2,1,0:T(8,128)(2,1)} %get-tuple-element.194.refs_0_, bf16[16,512,128]{2,1,0:T(8,128)(2,1)} %copy-done.64, bf16[16,512,128]{2,1,0:T(8,128)(2,1)} %get-tuple-element.195.refs_2_, ...), custom_call_target="tpu_custom_call" | custom-call | flops 10000000000 | bytes 100000000 | tf_op jit(solution)/shard_map/pallas_call | solution.py:152
  316.0 24.6 %shard_map.115 = (bf16[64,512,512]{2,1,0:T(8,128)(2,1)}, bf16[64,512,512]{2,1,0:T(8,128)(2,1)}) custom-call(s32[2]{0:T(128)} %pad_add_fusion.id_ref, bf16[16,512,128]{2,1,0:T(8,128)(2,1)} %copy-done.9, bf16[16,512,128]{2,1,0:T(8,128)(2,1)} %copy-done.14, bf16[16,512,128]{2,1,0:T(8,128)(2,1)} %copy-done.10, ...), custom_call_target="tpu_custom_call", output_to_operand_aliasing={{0}: (10, {}), {1}: (11, {})} | custom-call | flops 10000000000 | bytes 100000000 | tf_op jit(solution)/shard_map/pallas_call | solution.py:152
  341.2 24.6 %shard_map.116 = (bf16[64,512,512]{2,1,0:T(8,128)(2,1)}, bf16[64,512,512]{2,1,0:T(8,128)(2,1)}) custom-call(s32[2]{0:T(128)} %pad_add_fusion.id_ref, bf16[16,512,128]{2,1,0:T(8,128)(2,1)} %collective-permute-done.24.refs_0_, bf16[16,512,128]{2,1,0:T(8,128)(2,1)} %collective-permute-done.25.refs_1_, ...), custom_call_target="tpu_custom_call", output_to_operand_aliasing={{0}: (10, {}), {1}: (11, {})} | custom-call | flops 10000000000 | bytes 100000000 | tf_op jit(solution)/shard_map/pallas_call | solution.py:152
  366.4 24.7 %shard_map.117 = (bf16[64,512,512]{2,1,0:T(8,128)(2,1)}, bf16[64,512,512]{2,1,0:T(8,128)(2,1)}) custom-call(s32[2]{0:T(128)} %pad_add_fusion.id_ref, bf16[16,512,128]{2,1,0:T(8,128)(2,1)} %collective-permute-done.refs_0_, bf16[16,512,128]{2,1,0:T(8,128)(2,1)} %collective-permute-done.21.refs_1_, ...), custom_call_target="tpu_custom_call", output_to_operand_aliasing={{0}: (10, {}), {1}: (11, {})} | custom-call | flops 10000000000 | bytes 100000000 | tf_op jit(solution)/shard_map/pallas_call | solution.py:152
  393.4 24.7 %shard_map.118 = (bf16[64,512,512]{2,1,0:T(8,128)(2,1)}, bf16[64,512,512]{2,1,0:T(8,128)(2,1)}) custom-call(s32[2]{0:T(128)} %pad_add_fusion.id_ref, bf16[16,512,128]{2,1,0:T(8,128)(2,1)} %collective-permute-done.14.refs_0_, bf16[16,512,128]{2,1,0:T(8,128)(2,1)} %collective-permute-done.15.refs_1_, ...), custom_call_target="tpu_custom_call", output_to_operand_aliasing={{0}: (10, {}), {1}: (11, {})} | custom-call | flops 10000000000 | bytes 100000000 | tf_op jit(solution)/shard_map/pallas_call | solution.py:152
  418.7 24.6 %shard_map.119 = (bf16[64,512,512]{2,1,0:T(8,128)(2,1)}, bf16[64,512,512]{2,1,0:T(8,128)(2,1)}) custom-call(s32[2]{0:T(128)} %pad_add_fusion.id_ref, bf16[16,512,128]{2,1,0:T(8,128)(2,1)} %collective-permute-done.9.refs_0_, bf16[16,512,128]{2,1,0:T(8,128)(2,1)} %collective-permute-done.10.refs_1_, ...), custom_call_target="tpu_custom_call", output_to_operand_aliasing={{0}: (10, {}), {1}: (11, {})} | custom-call | flops 10000000000 | bytes 100000000 | tf_op jit(solution)/shard_map/pallas_call | solution.py:152
  443.3 24.6 %shard_map.120 = (bf16[64,512,512]{2,1,0:T(8,128)(2,1)}, bf16[64,512,512]{2,1,0:T(8,128)(2,1)}) custom-call(s32[2]{0:T(128)} %pad_add_fusion.id_ref, bf16[16,512,128]{2,1,0:T(8,128)(2,1)} %collective-permute-done.1.refs_0_, bf16[16,512,128]{2,1,0:T(8,128)(2,1)} %collective-permute-done.2.refs_1_, ...), custom_call_target="tpu_custom_call", output_to_operand_aliasing={{0}: (10, {}), {1}: (11, {})} | custom-call | flops 10000000000 | bytes 100000000 | tf_op jit(solution)/shard_map/pallas_call | solution.py:152
  594.9 35.3 %collective-permute-done.43.refs_0_ = bf16[16,512,128]{2,1,0:T(8,128)(2,1)S(1)} collective-permute-done((bf16[16,512,128]{2,1,0:T(8,128)(2,1)}, bf16[16,512,128]{2,1,0:T(8,128)(2,1)S(1)}, u32[]{:S(2)}, u32[]{:S(2)}) %collective-permute-start.43) | collective-permute-done | bytes 2097184 | tf_op jit(solution)/shard_map/ppermute | solution.py:478
  634.7 40.5 %collective-permute-done.55.refs_0_ = bf16[16,512,128]{2,1,0:T(8,128)(2,1)} collective-permute-done((bf16[16,512,128]{2,1,0:T(8,128)(2,1)}, bf16[16,512,128]{2,1,0:T(8,128)(2,1)}, u32[]{:S(2)}, u32[]{:S(2)}) %collective-permute-start.55) | collective-permute-done | bytes 2097184 | tf_op jit(solution)/shard_map/ppermute | solution.py:478
  678.7 41.5 %collective-permute-done.37.refs_0_ = bf16[16,512,128]{2,1,0:T(8,128)(2,1)} collective-permute-done((bf16[16,512,128]{2,1,0:T(8,128)(2,1)}, bf16[16,512,128]{2,1,0:T(8,128)(2,1)}, u32[]{:S(2)}, u32[]{:S(2)}) %collective-permute-start.37) | collective-permute-done | bytes 2097184 | tf_op jit(solution)/shard_map/ppermute | solution.py:478
  723.6 40.7 %collective-permute-done.49.refs_0_ = bf16[16,512,128]{2,1,0:T(8,128)(2,1)} collective-permute-done((bf16[16,512,128]{2,1,0:T(8,128)(2,1)}, bf16[16,512,128]{2,1,0:T(8,128)(2,1)}, u32[]{:S(2)}, u32[]{:S(2)}) %collective-permute-start.49) | collective-permute-done | bytes 2097184 | tf_op jit(solution)/shard_map/ppermute | solution.py:478
  776.3 45.0 %shard_map.127 = (bf16[64,512,512]{2,1,0:T(8,128)(2,1)}, bf16[64,512,512]{2,1,0:T(8,128)(2,1)}) custom-call(s32[2]{0:T(128)} %pad_add_fusion.id_ref, bf16[16,512,128]{2,1,0:T(8,128)(2,1)} %get-tuple-element.223.refs_0_, bf16[16,512,128]{2,1,0:T(8,128)(2,1)} %copy-done.67, bf16[16,512,128]{2,1,0:T(8,128)(2,1)} %get-tuple-element.224.refs_2_, ...), custom_call_target="tpu_custom_call" | custom-call | flops 10000000000 | bytes 100000000 | tf_op jit(solution)/shard_map/pallas_call | solution.py:152
  821.4 24.6 %shard_map.128 = (bf16[64,512,512]{2,1,0:T(8,128)(2,1)}, bf16[64,512,512]{2,1,0:T(8,128)(2,1)}) custom-call(s32[2]{0:T(128)} %pad_add_fusion.id_ref, bf16[16,512,128]{2,1,0:T(8,128)(2,1)} %copy-done.12, bf16[16,512,128]{2,1,0:T(8,128)(2,1)} %copy-done.16, bf16[16,512,128]{2,1,0:T(8,128)(2,1)} %copy-done.13, ...), custom_call_target="tpu_custom_call", output_to_operand_aliasing={{0}: (10, {}), {1}: (11, {})} | custom-call | flops 10000000000 | bytes 100000000 | tf_op jit(solution)/shard_map/pallas_call | solution.py:152
  846.6 24.6 %shard_map.129 = (bf16[64,512,512]{2,1,0:T(8,128)(2,1)}, bf16[64,512,512]{2,1,0:T(8,128)(2,1)}) custom-call(s32[2]{0:T(128)} %pad_add_fusion.id_ref, bf16[16,512,128]{2,1,0:T(8,128)(2,1)} %collective-permute-done.55.refs_0_, bf16[16,512,128]{2,1,0:T(8,128)(2,1)} %collective-permute-done.56.refs_1_, ...), custom_call_target="tpu_custom_call", output_to_operand_aliasing={{0}: (10, {}), {1}: (11, {})} | custom-call | flops 10000000000 | bytes 100000000 | tf_op jit(solution)/shard_map/pallas_call | solution.py:152
  871.7 24.6 %shard_map.130 = (bf16[64,512,512]{2,1,0:T(8,128)(2,1)}, bf16[64,512,512]{2,1,0:T(8,128)(2,1)}) custom-call(s32[2]{0:T(128)} %pad_add_fusion.id_ref, bf16[16,512,128]{2,1,0:T(8,128)(2,1)} %collective-permute-done.37.refs_0_, bf16[16,512,128]{2,1,0:T(8,128)(2,1)} %collective-permute-done.52.refs_1_, ...), custom_call_target="tpu_custom_call", output_to_operand_aliasing={{0}: (10, {}), {1}: (11, {})} | custom-call | flops 10000000000 | bytes 100000000 | tf_op jit(solution)/shard_map/pallas_call | solution.py:152
  896.4 24.6 %shard_map.131 = (bf16[64,512,512]{2,1,0:T(8,128)(2,1)}, bf16[64,512,512]{2,1,0:T(8,128)(2,1)}) custom-call(s32[2]{0:T(128)} %pad_add_fusion.id_ref, bf16[16,512,128]{2,1,0:T(8,128)(2,1)} %collective-permute-done.49.refs_0_, bf16[16,512,128]{2,1,0:T(8,128)(2,1)} %collective-permute-done.50.refs_1_, ...), custom_call_target="tpu_custom_call", output_to_operand_aliasing={{0}: (10, {}), {1}: (11, {})} | custom-call | flops 10000000000 | bytes 100000000 | tf_op jit(solution)/shard_map/pallas_call | solution.py:152
  921.0 24.6 %shard_map.132 = (bf16[64,512,512]{2,1,0:T(8,128)(2,1)}, bf16[64,512,512]{2,1,0:T(8,128)(2,1)}) custom-call(s32[2]{0:T(128)} %pad_add_fusion.id_ref, bf16[16,512,128]{2,1,0:T(8,128)(2,1)} %collective-permute-done.44.refs_0_, bf16[16,512,128]{2,1,0:T(8,128)(2,1)} %collective-permute-done.45.refs_1_, ...), custom_call_target="tpu_custom_call", output_to_operand_aliasing={{0}: (10, {}), {1}: (11, {})} | custom-call | flops 10000000000 | bytes 100000000 | tf_op jit(solution)/shard_map/pallas_call | solution.py:152
  945.7 24.6 %shard_map.133 = (bf16[64,512,512]{2,1,0:T(8,128)(2,1)}, bf16[64,512,512]{2,1,0:T(8,128)(2,1)}) custom-call(s32[2]{0:T(128)} %pad_add_fusion.id_ref, bf16[16,512,128]{2,1,0:T(8,128)(2,1)} %collective-permute-done.38.refs_0_, bf16[16,512,128]{2,1,0:T(8,128)(2,1)} %collective-permute-done.39.refs_1_, ...), custom_call_target="tpu_custom_call", output_to_operand_aliasing={{0}: (10, {}), {1}: (11, {})} | custom-call | flops 10000000000 | bytes 100000000 | tf_op jit(solution)/shard_map/pallas_call | solution.py:152
  1013.0 27.8 %shard_map.136 = (bf16[32,512,128]{2,1,0:T(8,128)(2,1)}, bf16[64,32,512]{2,1,0:T(8,128)(2,1)}, bf16[64,32,512]{2,1,0:T(8,128)(2,1)}, bf16[64,32,128]{2,1,0:T(8,1...) custom-call(s32[2]{0:T(128)} %pad_add_fusion.id_ref, ...), custom_call_target="tpu_custom_call" | custom-call | flops 10000000000 | bytes 100000000 | tf_op jit(solution)/shard_map/pallas_call | solution.py:381
  1040.8 28.0 %shard_map.137 = (bf16[32,512,128]{2,1,0:T(8,128)(2,1)}, bf16[64,32,512]{2,1,0:T(8,128)(2,1)}, bf16[64,32,512]{2,1,0:T(8,128)(2,1)}, bf16[64,32,128]{2,1,0:T(8,1...) custom-call(s32[2]{0:T(128)} %pad_add_fusion.id_ref, ...), custom_call_target="tpu_custom_call" | custom-call | flops 10000000000 | bytes 100000000 | tf_op jit(solution)/shard_map/pallas_call | solution.py:381
  1097.6 27.0 %collective-permute-done.87.rest_13_ = bf16[64,32,128]{2,1,0:T(8,128)(2,1)} collective-permute-done((bf16[64,32,128]{2,1,0:T(8,128)(2,1)}, bf16[64,32,128]{2,1,0:T(8,128)(2,1)}, u32[]{:S(2)}, u32[]{:S(2)}) %collective-permute-start.87) | collective-permute-done | bytes 524320 | tf_op jit(solution)/shard_map/ppermute | solution.py:478
  1316.1 41.2 %shard_map.142 = (f32[32,512,128]{2,1,0:T(8,128)}, f32[512,128]{1,0:T(8,128)}, f32[128,128]{1,0:T(8,128)}, f32[8,128]{1,0:T(8,128)}, f32[8,128]{1,0:T(8,128)}) custom-call(s32[2]{0:T(128)} %pad_add_fusion.id_ref, bf16[64,32,128]{2,1,0:T(8,128)(2,1)} %get-tuple-element.248.rest_16_.refs_0_, bf16[64,32,128]{2,1,0:T(8,128)(2,1)} %collective-permute-done.69.refs_1_, ...), custom_call_target="tpu_custom_call" | custom-call | flops 20000000000 | bytes 200000000 | tf_op jit(solution)/shard_map/pallas_call | solution.py:461
  1361.2 27.6 %shard_map.143 = (bf16[32,512,128]{2,1,0:T(8,128)(2,1)}, bf16[64,32,512]{2,1,0:T(8,128)(2,1)}, bf16[64,32,512]{2,1,0:T(8,128)(2,1)}, bf16[64,32,128]{2,1,0:T(8,1...) custom-call(s32[2]{0:T(128)} %pad_add_fusion.id_ref, ...), custom_call_target="tpu_custom_call" | custom-call | flops 10000000000 | bytes 100000000 | tf_op jit(solution)/shard_map/pallas_call | solution.py:381
  1394.6 41.2 %shard_map.144 = (f32[32,512,128]{2,1,0:T(8,128)}, f32[512,128]{1,0:T(8,128)}, f32[128,128]{1,0:T(8,128)}, f32[8,128]{1,0:T(8,128)}, f32[8,128]{1,0:T(8,128)}) custom-call(s32[2]{0:T(128)} %pad_add_fusion.id_ref, bf16[64,32,128]{2,1,0:T(8,128)(2,1)} %get-tuple-element.282.rest_16_.refs_0_, bf16[64,32,128]{2,1,0:T(8,128)(2,1)} %collective-permute-done.98.refs_1_, ...), custom_call_target="tpu_custom_call" | custom-call | flops 20000000000 | bytes 200000000 | tf_op jit(solution)/shard_map/pallas_call | solution.py:461
  1435.9 28.0 %shard_map.145 = (bf16[32,512,128]{2,1,0:T(8,128)(2,1)}, bf16[64,32,512]{2,1,0:T(8,128)(2,1)}, bf16[64,32,512]{2,1,0:T(8,128)(2,1)}, bf16[64,32,128]{2,1,0:T(8,1...) custom-call(s32[2]{0:T(128)} %pad_add_fusion.id_ref, ...), custom_call_target="tpu_custom_call" | custom-call | flops 10000000000 | bytes 100000000 | tf_op jit(solution)/shard_map/pallas_call | solution.py:381
  1492.5 26.8 %collective-permute-done.125.rest_13_ = bf16[64,32,128]{2,1,0:T(8,128)(2,1)S(1)} collective-permute-done((bf16[64,32,128]{2,1,0:T(8,128)(2,1)}, bf16[64,32,128]{2,1,0:T(8,128)(2,1)S(1)}, u32[]{:S(2)}, u32[]{:S(2)}) %collective-permute-start.125) | collective-permute-done | bytes 524320 | tf_op jit(solution)/shard_map/ppermute | solution.py:478
  1635.7 40.7 %shard_map.148 = (f32[64,512,128]{2,1,0:T(8,128)}, f32[512,128]{1,0:T(8,128)}, f32[128,128]{1,0:T(8,128)}, f32[8,128]{1,0:T(8,128)}, f32[8,128]{1,0:T(8,128)}) custom-call(s32[2]{0:T(128)} %pad_add_fusion.id_ref, bf16[64,64,512]{2,1,0:T(8,128)(2,1)} %get-tuple-element.305.rest_16_.refs_0_, bf16[64,64,512]{2,1,0:T(8,128)(2,1)} %collective-permute-done.113.refs_1_, ...), custom_call_target="tpu_custom_call" | custom-call | flops 20000000000 | bytes 200000000 | tf_op jit(solution)/shard_map/pallas_call | solution.py:461
  1676.4 40.8 %shard_map.149 = (f32[64,512,128]{2,1,0:T(8,128)}, f32[512,128]{1,0:T(8,128)}, f32[128,128]{1,0:T(8,128)}, f32[8,128]{1,0:T(8,128)}, f32[8,128]{1,0:T(8,128)}) custom-call(s32[2]{0:T(128)} %pad_add_fusion.id_ref, bf16[64,64,512]{2,1,0:T(8,128)(2,1)} %get-tuple-element.305.rest_16_.refs_0_, ...), custom_call_target="tpu_custom_call", output_to_operand_aliasing={{0}: (13, {})} | custom-call | flops 20000000000 | bytes 200000000 | tf_op jit(solution)/shard_map/pallas_call | solution.py:461
  (526 shorter events, 696.3 us)
Async XLA Ops:
  78.5 93.6 %collective-permute-start.11 = (bf16[16,512,128]{2,1,0:T(8,128)(2,1)}, bf16[16,512,128]{2,1,0:T(8,128)(2,1)}, u32[]{:S(2)}, u32[]{:S(2)}) collective-permute-start(bf16[16,512,128]{2,1,0:T(8,128)(2,1)} %get-tuple-element.195.refs_2_), channel_id=1, source_target_pairs={{0,4},{1,5},{2,6},{3,7},{4,0},{5,1},{6,2},{7,3}} | collective-permute-start | bytes 6291464 | tf_op jit(solution)/shard_map/ppermute | solution.py:478
  80.4 92.9 %collective-permute-start.24 = (bf16[16,512,128]{2,1,0:T(8,128)(2,1)}, bf16[16,512,128]{2,1,0:T(8,128)(2,1)}, u32[]{:S(2)}, u32[]{:S(2)}) collective-permute-start(bf16[16,512,128]{2,1,0:T(8,128)(2,1)} %get-tuple-element.195.refs_2_), channel_id=1, source_target_pairs={{0,2},{1,3},{2,0},{3,1},{4,6},{5,7},{6,4},{7,5}} | collective-permute-start | bytes 6291464 | tf_op jit(solution)/shard_map/ppermute | solution.py:478
  81.5 134.6 %collective-permute-start = (bf16[16,512,128]{2,1,0:T(8,128)(2,1)}, bf16[16,512,128]{2,1,0:T(8,128)(2,1)}, u32[]{:S(2)}, u32[]{:S(2)}) collective-permute-start(bf16[16,512,128]{2,1,0:T(8,128)(2,1)} %get-tuple-element.191.refs_4_), channel_id=1, source_target_pairs={{0,2},{1,3},{2,0},{3,1},{4,6},{5,7},{6,4},{7,5}} | collective-permute-start | bytes 6291464 | tf_op jit(solution)/shard_map/ppermute | solution.py:478
  126.2 90.9 %collective-permute-start.22 = (bf16[16,512,128]{2,1,0:T(8,128)(2,1)}, bf16[16,512,128]{2,1,0:T(8,128)(2,1)}, u32[]{:S(2)}, u32[]{:S(2)}) collective-permute-start(bf16[16,512,128]{2,1,0:T(8,128)(2,1)} %get-tuple-element.191.refs_4_), channel_id=1, source_target_pairs={{0,4},{1,5},{2,6},{3,7},{4,0},{5,1},{6,2},{7,3}} | collective-permute-start | bytes 6291464 | tf_op jit(solution)/shard_map/ppermute | solution.py:478
  127.1 132.9 %collective-permute-start.3 = (bf16[16,512,128]{2,1,0:T(8,128)(2,1)}, bf16[16,512,128]{2,1,0:T(8,128)(2,1)}, u32[]{:S(2)}, u32[]{:S(2)}) collective-permute-start(bf16[16,512,128]{2,1,0:T(8,128)(2,1)} %get-tuple-element.193.refs_6_), channel_id=1, source_target_pairs={{0,4},{1,5},{2,6},{3,7},{4,0},{5,1},{6,2},{7,3}} | collective-permute-start | bytes 6291464 | tf_op jit(solution)/shard_map/ppermute | solution.py:478
  172.1 87.9 %collective-permute-start.14 = (bf16[16,512,128]{2,1,0:T(8,128)(2,1)}, bf16[16,512,128]{2,1,0:T(8,128)(2,1)}, u32[]{:S(2)}, u32[]{:S(2)}) collective-permute-start(bf16[16,512,128]{2,1,0:T(8,128)(2,1)} %get-tuple-element.193.refs_6_), channel_id=1, source_target_pairs={{0,2},{1,3},{2,0},{3,1},{4,6},{5,7},{6,4},{7,5}} | collective-permute-start | bytes 6291464 | tf_op jit(solution)/shard_map/ppermute | solution.py:478
  173.3 87.3 %collective-permute-start.27 = (bf16[16,512,128]{2,1,0:T(8,128)(2,1)S(1)}, bf16[16,512,128]{2,1,0:T(8,128)(2,1)S(1)}, u32[]{:S(2)}, u32[]{:S(2)}) collective-permute-start(bf16[16,512,128]{2,1,0:T(8,128)(2,1)S(1)} %collective-permute-done.8.refs_0_), channel_id=1, source_target_pairs={{0,1},{1,0},{2,3},{3,2},{4,5},{5,4},{6,7},{7,6}} | collective-permute-start | bytes 6291464 | tf_op jit(solution)/shard_map/ppermute | solution.py:478
  264.0 76.6 %collective-permute-start.12 = (bf16[16,512,128]{2,1,0:T(8,128)(2,1)}, bf16[16,512,128]{2,1,0:T(8,128)(2,1)}, u32[]{:S(2)}, u32[]{:S(2)}) collective-permute-start(bf16[16,512,128]{2,1,0:T(8,128)(2,1)} %collective-permute-done.11.refs_2_), channel_id=1, source_target_pairs={{0,2},{1,3},{2,0},{3,1},{4,6},{5,7},{6,4},{7,5}} | collective-permute-start | bytes 6291464 | tf_op jit(solution)/shard_map/ppermute | solution.py:478
  265.2 76.0 %collective-permute-start.9 = (bf16[16,512,128]{2,1,0:T(8,128)(2,1)}, bf16[16,512,128]{2,1,0:T(8,128)(2,1)}, u32[]{:S(2)}, u32[]{:S(2)}) collective-permute-start(bf16[16,512,128]{2,1,0:T(8,128)(2,1)} %copy-done.9), channel_id=1, source_target_pairs={{0,4},{1,5},{2,6},{3,7},{4,0},{5,1},{6,2},{7,3}} | collective-permute-start | bytes 6291464 | tf_op jit(solution)/shard_map/ppermute | solution.py:478
  267.5 98.3 %collective-permute-start.4 = (bf16[16,512,128]{2,1,0:T(8,128)(2,1)}, bf16[16,512,128]{2,1,0:T(8,128)(2,1)}, u32[]{:S(2)}, u32[]{:S(2)}) collective-permute-start(bf16[16,512,128]{2,1,0:T(8,128)(2,1)} %collective-permute-done.3.refs_2_), channel_id=1, source_target_pairs={{0,2},{1,3},{2,0},{3,1},{4,6},{5,7},{6,4},{7,5}} | collective-permute-start | bytes 6291464 | tf_op jit(solution)/shard_map/ppermute | solution.py:478
  270.5 95.8 %collective-permute-start.1 = (bf16[16,512,128]{2,1,0:T(8,128)(2,1)}, bf16[16,512,128]{2,1,0:T(8,128)(2,1)}, u32[]{:S(2)}, u32[]{:S(2)}) collective-permute-start(bf16[16,512,128]{2,1,0:T(8,128)(2,1)} %collective-permute-done.refs_0_), channel_id=1, source_target_pairs={{0,4},{1,5},{2,6},{3,7},{4,0},{5,1},{6,2},{7,3}} | collective-permute-start | bytes 6291464 | tf_op jit(solution)/shard_map/ppermute | solution.py:478
  316.0 75.2 %collective-permute-start.15 = (bf16[16,512,128]{2,1,0:T(8,128)(2,1)}, bf16[16,512,128]{2,1,0:T(8,128)(2,1)}, u32[]{:S(2)}, u32[]{:S(2)}) collective-permute-start(bf16[16,512,128]{2,1,0:T(8,128)(2,1)} %collective-permute-done.14.refs_0_), channel_id=1, source_target_pairs={{0,1},{1,0},{2,3},{3,2},{4,5},{5,4},{6,7},{7,6}} | collective-permute-start | bytes 6291464 | tf_op jit(solution)/shard_map/ppermute | solution.py:478
  340.6 77.5 %collective-permute-start.13 = (bf16[16,512,128]{2,1,0:T(8,128)(2,1)}, bf16[16,512,128]{2,1,0:T(8,128)(2,1)}, u32[]{:S(2)}, u32[]{:S(2)}) collective-permute-start(bf16[16,512,128]{2,1,0:T(8,128)(2,1)} %collective-permute-done.12.refs_2_), channel_id=1, source_target_pairs={{0,1},{1,0},{2,3},{3,2},{4,5},{5,4},{6,7},{7,6}} | collective-permute-start | bytes 6291464 | tf_op jit(solution)/shard_map/ppermute | solution.py:478
  341.2 76.9 %collective-permute-start.10 = (bf16[16,512,128]{2,1,0:T(8,128)(2,1)}, bf16[16,512,128]{2,1,0:T(8,128)(2,1)}, u32[]{:S(2)}, u32[]{:S(2)}) collective-permute-start(bf16[16,512,128]{2,1,0:T(8,128)(2,1)} %collective-permute-done.9.refs_0_), channel_id=1, source_target_pairs={{0,1},{1,0},{2,3},{3,2},{4,5},{5,4},{6,7},{7,6}} | collective-permute-start | bytes 6291464 | tf_op jit(solution)/shard_map/ppermute | solution.py:478
  365.9 77.5 %collective-permute-start.5 = (bf16[16,512,128]{2,1,0:T(8,128)(2,1)}, bf16[16,512,128]{2,1,0:T(8,128)(2,1)}, u32[]{:S(2)}, u32[]{:S(2)}) collective-permute-start(bf16[16,512,128]{2,1,0:T(8,128)(2,1)} %collective-permute-done.4.refs_2_), channel_id=1, source_target_pairs={{0,1},{1,0},{2,3},{3,2},{4,5},{5,4},{6,7},{7,6}} | collective-permute-start | bytes 6291464 | tf_op jit(solution)/shard_map/ppermute | solution.py:478
  366.3 77.0 %collective-permute-start.2 = (bf16[16,512,128]{2,1,0:T(8,128)(2,1)}, bf16[16,512,128]{2,1,0:T(8,128)(2,1)}, u32[]{:S(2)}, u32[]{:S(2)}) collective-permute-start(bf16[16,512,128]{2,1,0:T(8,128)(2,1)} %collective-permute-done.1.refs_0_), channel_id=1, source_target_pairs={{0,1},{1,0},{2,3},{3,2},{4,5},{5,4},{6,7},{7,6}} | collective-permute-start | bytes 6291464 | tf_op jit(solution)/shard_map/ppermute | solution.py:478
  587.9 87.4 %collective-permute-start.55 = (bf16[16,512,128]{2,1,0:T(8,128)(2,1)}, bf16[16,512,128]{2,1,0:T(8,128)(2,1)}, u32[]{:S(2)}, u32[]{:S(2)}) collective-permute-start(bf16[16,512,128]{2,1,0:T(8,128)(2,1)} %get-tuple-element.224.refs_2_), channel_id=1, source_target_pairs={{0,2},{1,3},{2,0},{3,1},{4,6},{5,7},{6,4},{7,5}} | collective-permute-start | bytes 6291464 | tf_op jit(solution)/shard_map/ppermute | solution.py:478
  590.9 87.9 %collective-permute-start.46 = (bf16[16,512,128]{2,1,0:T(8,128)(2,1)}, bf16[16,512,128]{2,1,0:T(8,128)(2,1)}, u32[]{:S(2)}, u32[]{:S(2)}) collective-permute-start(bf16[16,512,128]{2,1,0:T(8,128)(2,1)} %get-tuple-element.224.refs_2_), channel_id=1, source_target_pairs={{0,4},{1,5},{2,6},{3,7},{4,0},{5,1},{6,2},{7,3}} | collective-permute-start | bytes 6291464 | tf_op jit(solution)/shard_map/ppermute | solution.py:478
  593.9 126.4 %collective-permute-start.37 = (bf16[16,512,128]{2,1,0:T(8,128)(2,1)}, bf16[16,512,128]{2,1,0:T(8,128)(2,1)}, u32[]{:S(2)}, u32[]{:S(2)}) collective-permute-start(bf16[16,512,128]{2,1,0:T(8,128)(2,1)} %get-tuple-element.219.refs_4_), channel_id=1, source_target_pairs={{0,2},{1,3},{2,0},{3,1},{4,6},{5,7},{6,4},{7,5}} | collective-permute-start | bytes 6291464 | tf_op jit(solution)/shard_map/ppermute | solution.py:478
  630.2 93.4 %collective-permute-start.53 = (bf16[16,512,128]{2,1,0:T(8,128)(2,1)}, bf16[16,512,128]{2,1,0:T(8,128)(2,1)S(1)}, u32[]{:S(2)}, u32[]{:S(2)}) collective-permute-start(bf16[16,512,128]{2,1,0:T(8,128)(2,1)} %get-tuple-element.219.refs_4_), channel_id=1, source_target_pairs={{0,4},{1,5},{2,6},{3,7},{4,0},{5,1},{6,2},{7,3}} | collective-permute-start | bytes 6291464 | tf_op jit(solution)/shard_map/ppermute | solution.py:478
  633.7 130.6 %collective-permute-start.49 = (bf16[16,512,128]{2,1,0:T(8,128)(2,1)}, bf16[16,512,128]{2,1,0:T(8,128)(2,1)}, u32[]{:S(2)}, u32[]{:S(2)}) collective-permute-start(bf16[16,512,128]{2,1,0:T(8,128)(2,1)} %get-tuple-element.222.refs_6_), channel_id=1, source_target_pairs={{0,2},{1,3},{2,0},{3,1},{4,6},{5,7},{6,4},{7,5}} | collective-permute-start | bytes 6291464 | tf_op jit(solution)/shard_map/ppermute | solution.py:478
  675.3 92.5 %collective-permute-start.40 = (bf16[16,512,128]{2,1,0:T(8,128)(2,1)}, bf16[16,512,128]{2,1,0:T(8,128)(2,1)}, u32[]{:S(2)}, u32[]{:S(2)}) collective-permute-start(bf16[16,512,128]{2,1,0:T(8,128)(2,1)} %get-tuple-element.222.refs_6_), channel_id=1, source_target_pairs={{0,4},{1,5},{2,6},{3,7},{4,0},{5,1},{6,2},{7,3}} | collective-permute-start | bytes 6291464 | tf_op jit(solution)/shard_map/ppermute | solution.py:478
  678.7 89.1 %collective-permute-start.58 = (bf16[16,512,128]{2,1,0:T(8,128)(2,1)S(1)}, bf16[16,512,128]{2,1,0:T(8,128)(2,1)S(1)}, u32[]{:S(2)}, u32[]{:S(2)}) collective-permute-start(bf16[16,512,128]{2,1,0:T(8,128)(2,1)S(1)} %collective-permute-done.43.refs_0_), channel_id=1, source_target_pairs={{0,1},{1,0},{2,3},{3,2},{4,5},{5,4},{6,7},{7,6}} | collective-permute-start | bytes 6291464 | tf_op jit(solution)/shard_map/ppermute | solution.py:478
  770.0 76.0 %collective-permute-start.47 = (bf16[16,512,128]{2,1,0:T(8,128)(2,1)}, bf16[16,512,128]{2,1,0:T(8,128)(2,1)}, u32[]{:S(2)}, u32[]{:S(2)}) collective-permute-start(bf16[16,512,128]{2,1,0:T(8,128)(2,1)} %collective-permute-done.46.refs_2_), channel_id=1, source_target_pairs={{0,2},{1,3},{2,0},{3,1},{4,6},{5,7},{6,4},{7,5}} | collective-permute-start | bytes 6291464 | tf_op jit(solution)/shard_map/ppermute | solution.py:478
  771.0 75.5 %collective-permute-start.44 = (bf16[16,512,128]{2,1,0:T(8,128)(2,1)}, bf16[16,512,128]{2,1,0:T(8,128)(2,1)}, u32[]{:S(2)}, u32[]{:S(2)}) collective-permute-start(bf16[16,512,128]{2,1,0:T(8,128)(2,1)} %copy-done.12), channel_id=1, source_target_pairs={{0,4},{1,5},{2,6},{3,7},{4,0},{5,1},{6,2},{7,3}} | collective-permute-start | bytes 6291464 | tf_op jit(solution)/shard_map/ppermute | solution.py:478
  772.3 99.4 %collective-permute-start.38 = (bf16[16,512,128]{2,1,0:T(8,128)(2,1)}, bf16[16,512,128]{2,1,0:T(8,128)(2,1)}, u32[]{:S(2)}, u32[]{:S(2)}) collective-permute-start(bf16[16,512,128]{2,1,0:T(8,128)(2,1)} %collective-permute-done.37.refs_0_), channel_id=1, source_target_pairs={{0,4},{1,5},{2,6},{3,7},{4,0},{5,1},{6,2},{7,3}} | collective-permute-start | bytes 6291464 | tf_op jit(solution)/shard_map/ppermute | solution.py:478
  775.3 95.9 %collective-permute-start.41 = (bf16[16,512,128]{2,1,0:T(8,128)(2,1)}, bf16[16,512,128]{2,1,0:T(8,128)(2,1)}, u32[]{:S(2)}, u32[]{:S(2)}) collective-permute-start(bf16[16,512,128]{2,1,0:T(8,128)(2,1)} %collective-permute-done.40.refs_2_), channel_id=1, source_target_pairs={{0,2},{1,3},{2,0},{3,1},{4,6},{5,7},{6,4},{7,5}} | collective-permute-start | bytes 6291464 | tf_op jit(solution)/shard_map/ppermute | solution.py:478
  821.4 75.0 %collective-permute-start.51 = (bf16[16,512,128]{2,1,0:T(8,128)(2,1)}, bf16[16,512,128]{2,1,0:T(8,128)(2,1)}, u32[]{:S(2)}, u32[]{:S(2)}) collective-permute-start(bf16[16,512,128]{2,1,0:T(8,128)(2,1)} %collective-permute-done.40.refs_2_), channel_id=1, source_target_pairs={{0,1},{1,0},{2,3},{3,2},{4,5},{5,4},{6,7},{7,6}} | collective-permute-start | bytes 6291464 | tf_op jit(solution)/shard_map/ppermute | solution.py:478
  846.0 75.0 %collective-permute-start.48 = (bf16[16,512,128]{2,1,0:T(8,128)(2,1)}, bf16[16,512,128]{2,1,0:T(8,128)(2,1)}, u32[]{:S(2)}, u32[]{:S(2)}) collective-permute-start(bf16[16,512,128]{2,1,0:T(8,128)(2,1)} %collective-permute-done.47.refs_2_), channel_id=1, source_target_pairs={{0,1},{1,0},{2,3},{3,2},{4,5},{5,4},{6,7},{7,6}} | collective-permute-start | bytes 6291464 | tf_op jit(solution)/shard_map/ppermute | solution.py:478
  846.5 74.5 %collective-permute-start.45 = (bf16[16,512,128]{2,1,0:T(8,128)(2,1)}, bf16[16,512,128]{2,1,0:T(8,128)(2,1)}, u32[]{:S(2)}, u32[]{:S(2)}) collective-permute-start(bf16[16,512,128]{2,1,0:T(8,128)(2,1)} %collective-permute-done.44.refs_0_), channel_id=1, source_target_pairs={{0,1},{1,0},{2,3},{3,2},{4,5},{5,4},{6,7},{7,6}} | collective-permute-start | bytes 6291464 | tf_op jit(solution)/shard_map/ppermute | solution.py:478
  871.2 74.4 %collective-permute-start.42 = (bf16[16,512,128]{2,1,0:T(8,128)(2,1)}, bf16[16,512,128]{2,1,0:T(8,128)(2,1)}, u32[]{:S(2)}, u32[]{:S(2)}) collective-permute-start(bf16[16,512,128]{2,1,0:T(8,128)(2,1)} %collective-permute-done.41.refs_2_), channel_id=1, source_target_pairs={{0,1},{1,0},{2,3},{3,2},{4,5},{5,4},{6,7},{7,6}} | collective-permute-start | bytes 6291464 | tf_op jit(solution)/shard_map/ppermute | solution.py:478
  871.7 74.0 %collective-permute-start.39 = (bf16[16,512,128]{2,1,0:T(8,128)(2,1)}, bf16[16,512,128]{2,1,0:T(8,128)(2,1)}, u32[]{:S(2)}, u32[]{:S(2)}) collective-permute-start(bf16[16,512,128]{2,1,0:T(8,128)(2,1)} %collective-permute-done.38.refs_0_), channel_id=1, source_target_pairs={{0,1},{1,0},{2,3},{3,2},{4,5},{5,4},{6,7},{7,6}} | collective-permute-start | bytes 6291464 | tf_op jit(solution)/shard_map/ppermute | solution.py:478
  (185 other events, 8020.2 us)
